TPU v7x, 512 devices: a whole 4x8x8 slice. The times are simulated.
512 devices in a mesh: dp: 8 (over z_hi, core), mp: 64 (over z_lo, x, y).
Axes of the slice: x: 4, y: 8, z: 8 (z_hi: 4, z_lo: 2; z = z_hi * 2 + z_lo), core: 2. Of those that a mesh axis runs over, the one named last changes fastest.
Arguments:
- inputs: bfloat16 [2048, 4096], P('dp'), may hold values from -6 to 6
- upstream: bfloat16 [2048, 4096], P('dp'), may hold values from -6 to 6
- eig_tiles: bfloat16 [64, 8, 2, 128, 128], P('mp'), may hold values from -0.09375 to 0.09375
- eigvals: float32 [4096], replicated, may hold values from 0.25 to 4
Outputs:
- grad_t: bfloat16 [4096, 2048], P('mp', 'dp')
All inputs are finite; a program needn't handle non-finite values.
Results may differ from a plain program's by a relative error of at most 0.013.
Values may be sent and summed in bfloat16 or wider, within the bound.
No kernel may reach another device: no remote copies, remote signals or barrier semaphores. Data moves between devices by JAX's collectives and lax.ppermute only.
A program may use at most 64 MiB of HBM per device.

v0:
```python
import jax
import jax.numpy as jnp
from jax import lax
from jax.sharding import PartitionSpec as P


def split_up(value, dim, length):
    dims = value.shape
    blocks = value.reshape(*dims[:dim], length, dims[dim] // length, *dims[dim + 1 :])
    return jnp.moveaxis(blocks, dim, 0)


def summed_on_arrival(value, axis, dim):
    length = lax.axis_size(axis)
    blocks = lax.all_to_all(split_up(value, dim, length), axis, 0, 0, tiled=True)
    return jnp.sum(blocks.astype(jnp.float32), axis=0)


def laid_out(blocks, dim):
    blocks = jnp.moveaxis(blocks, 0, dim)
    dims = blocks.shape
    return blocks.reshape(*dims[:dim], dims[dim] * dims[dim + 1], *dims[dim + 2 :])


def copy_for_each(value, axis):
    length = lax.axis_size(axis)
    return lax.all_to_all(
        jnp.broadcast_to(value[None], (length, *value.shape)), axis, 0, 0, tiled=True
    )


def gather_directly(value, axis, dim):
    return laid_out(copy_for_each(value, axis), dim)


def kernel_of(left, right):
    root_left = jnp.sqrt(left)[:, None]
    root_right = jnp.sqrt(right)[None, :]
    return -1.0 / (root_left * root_right * (root_left + root_right))


def on_device(inputs, upstream, eig_tiles, eigvals):
    groups = lax.axis_size("mp")
    member = lax.axis_index("mp")
    width = eigvals.shape[0]
    slab = width // groups
    tile_rows = eig_tiles.shape[1]
    tile_cols = eig_tiles.shape[2]
    tile = eig_tiles.shape[3]
    grid_rows = width // (tile_rows * tile)
    grid_cols = groups // grid_rows
    piece = tile_cols * tile // groups
    local = jnp.transpose(eig_tiles[0], (0, 2, 1, 3)).reshape(tile_rows * tile, groups, piece)
    moved = lax.all_to_all(local, "mp", split_axis=1, concat_axis=1, tiled=True)
    moved = moved.reshape(tile_rows, tile, grid_rows, grid_cols, piece)
    basis = jnp.transpose(moved, (0, 2, 1, 3, 4)).reshape(width, slab)
    ordered = jnp.transpose(eigvals.reshape(tile_cols, grid_cols, tile), (1, 0, 2)).reshape(
        grid_cols, groups, piece
    )
    ordered = jnp.transpose(ordered, (1, 0, 2)).reshape(width)
    own = lax.dynamic_slice_in_dim(ordered, member * slab, slab)
    proj_in = jnp.dot(inputs, basis, preferred_element_type=jnp.float32).astype(jnp.bfloat16)
    proj_up = jnp.dot(upstream, basis, preferred_element_type=jnp.float32).astype(jnp.bfloat16)
    stacked = jnp.stack([proj_in, proj_up], 0)
    over_tokens = (((0,), (0,)), ((), ()))
    pieces = lax.all_gather(stacked, "mp", axis=2, tiled=True)
    part_in = pieces[0]
    part_up = pieces[1]
    block = lax.dot_general(proj_in, part_up, over_tokens, preferred_element_type=jnp.float32)
    block = block + lax.dot_general(
        proj_up, part_in, over_tokens, preferred_element_type=jnp.float32
    )
    joined = jnp.concatenate([block, part_in.astype(jnp.float32)], 0)
    gram = joined[:slab]
    all_in = joined[slab:].astype(jnp.bfloat16)
    share = summed_on_arrival(gram.astype(jnp.bfloat16), "dp", 0)
    count = share.shape[0]
    own_part = lax.dynamic_slice_in_dim(own, lax.axis_index("dp") * count, count)
    part = (kernel_of(own_part, ordered) * (0.5 * share)).astype(jnp.bfloat16)
    weighted = gather_directly(part, "dp", 0)
    over_columns = (((1,), (1,)), ((), ()))
    mixed = lax.dot_general(all_in, weighted, over_columns, preferred_element_type=jnp.float32)
    factor = 2.0 / (lax.axis_size("dp") * inputs.shape[0])
    update = (proj_up.astype(jnp.float32) / jnp.sqrt(own)[None, :] + factor * mixed).astype(
        jnp.bfloat16
    )
    own_rows = lax.all_to_all(basis, "mp", split_axis=0, concat_axis=1, tiled=True)
    every_update = gather_directly(update, "mp", 1)
    result = lax.dot_general(
        own_rows, every_update, over_columns, preferred_element_type=jnp.float32
    )
    return result.astype(jnp.bfloat16)


def solution(mesh):
    return jax.shard_map(
        on_device,
        mesh=mesh,
        in_specs=(P("dp", None), P("dp", None), P("mp", None, None, None, None), P()),
        out_specs=P("mp", "dp"),
        check_vma=False,
    )
```

profile of v0, /device:TPU:8, one launch (start us, length us, event | category | flops | bytes accessed | tf_op | source)
XLA Modules:
  0.0 494.4 jit_solution(2258323800576001424)
XLA Ops:
  6.5 1.5 copy.11
  8.2 30.6 %all_to_all.36 = bf16[1024,64,4]{0,2,1:T(4,128)(2,1)S(1)} all-to-all(bf16[1024,64,4]{0,2,1:T(4,128)(2,1)S(1)} %reshape.93), channel_id=1, replica_groups=mesh['dp'=8,'mp'=64] {'mp'}, dimensions={1} | all-to-all | bytes 1048576 | tf_op jit(solution)/shard_map/all_to_all | solution.py:54
  38.7 1.0 reshape.102
  39.7 1.7 copy.13
  44.8 303.2 %all-gather.2.cloned.1.call-done = bf16[2,256,4096]{1,2,0:T(8,128)(2,1)} async-done(((bf16[2,256,64]{1,2,0:T(8,128)(2,1)}), bf16[2,256,4096]{1,2,0:T(8,128)(2,1)}) %all-gather.2.cloned.1.call-update) | async-done | bytes 4194320 | tf_op jit(solution)/shard_map/all_gather | solution.py:66
  348.1 2.3 fusion.2
  350.4 3.2 fusion.1
  353.6 6.8 %all-to-all-start.1 = ((bf16[8,8,4096]{2,1,0:T(8,128)(2,1)}), bf16[8,8,4096]{2,1,0:T(8,128)(2,1)S(1)}, u32[]{:S(2)}, u32[]{:S(2)}) async-start(bf16[8,8,4096]{2,1,0:T(8,128)(2,1)} %fusion.1), calls=%async_computation.1 | async-start | bytes 1048576 | tf_op jit(solution)/shard_map/all_to_all | solution.py:15
  360.5 1.2 copy.15
  361.8 1.3 reshape.98
  363.2 15.2 %all-to-all-done.1 = bf16[8,8,4096]{2,1,0:T(8,128)(2,1)S(1)} async-done(((bf16[8,8,4096]{2,1,0:T(8,128)(2,1)}), bf16[8,8,4096]{2,1,0:T(8,128)(2,1)S(1)}, u32[]{:S(2)}, u32[]{:S(2)}) %all-to-all-start.1) | async-done | bytes 524320 | tf_op jit(solution)/shard_map/all_to_all | solution.py:15
  379.4 3.5 all-to-all-start.2
  382.9 1.4 all_to_all.28
  384.3 2.9 copy.17
  387.3 3.0 reshape.103
  390.3 10.5 %all-to-all-done.2 = bf16[8,8,4096]{2,1,0:T(8,128)(2,1)S(1)} async-done(((bf16[8,8,4096]{2,1,0:T(8,128)(2,1)}), bf16[8,8,4096]{2,1,0:T(8,128)(2,1)S(1)}, u32[]{:S(2)}, u32[]{:S(2)}) %all-to-all-start.2) | async-done | bytes 524320 | tf_op jit(solution)/shard_map/all_to_all | solution.py:27
  400.8 8.2 %all-to-all-start.4 = ((bf16[64,2,2048]{2,1,0:T(2,128)(2,1)}), bf16[64,2,2048]{2,1,0:T(2,128)(2,1)S(1)}, u32[]{:S(2)}, u32[]{:S(2)}) async-start(bf16[64,2,2048]{2,1,0:T(2,128)(2,1)} %reshape.103), calls=%async_computation.4 | async-start | bytes 1048576 | tf_op jit(solution)/shard_map/all_to_all | solution.py:87
  409.1 2.1 fusion.11
  411.2 15.7 %all-to-all-done.4 = bf16[64,2,2048]{2,1,0:T(2,128)(2,1)S(1)} async-done(((bf16[64,2,2048]{2,1,0:T(2,128)(2,1)}), bf16[64,2,2048]{2,1,0:T(2,128)(2,1)S(1)}, u32[]{:S(2)}, u32[]{:S(2)}) %all-to-all-start.4) | async-done | bytes 524320 | tf_op jit(solution)/shard_map/all_to_all | solution.py:87
  426.9 1.6 broadcast_in_dim.5
  428.4 5.7 %all-to-all-start.3 = ((bf16[64,256,64]{1,2,0:T(8,128)(2,1)}), bf16[64,256,64]{1,2,0:T(8,128)(2,1)}, u32[]{:S(2)}, u32[]{:S(2)}) async-start(bf16[64,256,64]{1,2,0:T(8,128)(2,1)} %broadcast_in_dim.5), calls=%async_computation.3 | async-start | bytes 4194304 | tf_op jit(solution)/shard_map/all_to_all | solution.py:27
  434.2 1.6 reshape.104
  435.8 48.6 %all-to-all-done.3 = bf16[64,256,64]{1,2,0:T(8,128)(2,1)} async-done(((bf16[64,256,64]{1,2,0:T(8,128)(2,1)}), bf16[64,256,64]{1,2,0:T(8,128)(2,1)}, u32[]{:S(2)}, u32[]{:S(2)}) %all-to-all-start.3) | async-done | bytes 2097184 | tf_op jit(solution)/shard_map/all_to_all | solution.py:27
  484.5 3.0 fusion.15
  (20 shorter events, 4.8 us)
Async XLA Ops:
  6.5 35.3 %copy-start = (bf16[256,4096]{1,0:T(8,128)(2,1)S(1)}, bf16[256,4096]{1,0:T(8,128)(2,1)}, u32[]{:S(2)}) copy-start(bf16[256,4096]{1,0:T(8,128)(2,1)} %param.5) | copy-start | bytes 6291460
  6.5 341.5 %all-gather.2.cloned.1.call-start = ((), (), s32[]{:S(2)}) async-start(), calls=%async_computation.5 | async-start | bytes 4259840 | tf_op jit(solution)/shard_map/all_gather | solution.py:66
  41.8 1.6 copy-start.1
  350.4 10.0 %copy-start.2 = (f32[4096]{0:T(1024)S(1)}, f32[4096]{0:T(1024)}, u32[]{:S(2)}) copy-start(f32[4096]{0:T(1024)} %param.7) | copy-start | bytes 49156
  353.6 24.8 %all-to-all-start.1 = ((bf16[8,8,4096]{2,1,0:T(8,128)(2,1)}), bf16[8,8,4096]{2,1,0:T(8,128)(2,1)S(1)}, u32[]{:S(2)}, u32[]{:S(2)}) async-start(bf16[8,8,4096]{2,1,0:T(8,128)(2,1)} %fusion.1), calls=%async_computation.1 | async-start | bytes 1048576 | tf_op jit(solution)/shard_map/all_to_all | solution.py:15
  379.4 21.4 %all-to-all-start.2 = ((bf16[8,8,4096]{2,1,0:T(8,128)(2,1)}), bf16[8,8,4096]{2,1,0:T(8,128)(2,1)S(1)}, u32[]{:S(2)}, u32[]{:S(2)}) async-start(bf16[8,8,4096]{2,1,0:T(8,128)(2,1)} %broadcast_in_dim.4), calls=%async_computation.2 | async-start | bytes 1048576 | tf_op jit(solution)/shard_map/all_to_all | solution.py:27
  400.8 26.1 %all-to-all-start.4 = ((bf16[64,2,2048]{2,1,0:T(2,128)(2,1)}), bf16[64,2,2048]{2,1,0:T(2,128)(2,1)S(1)}, u32[]{:S(2)}, u32[]{:S(2)}) async-start(bf16[64,2,2048]{2,1,0:T(2,128)(2,1)} %reshape.103), calls=%async_computation.4 | async-start | bytes 1048576 | tf_op jit(solution)/shard_map/all_to_all | solution.py:87
  428.4 56.0 %all-to-all-start.3 = ((bf16[64,256,64]{1,2,0:T(8,128)(2,1)}), bf16[64,256,64]{1,2,0:T(8,128)(2,1)}, u32[]{:S(2)}, u32[]{:S(2)}) async-start(bf16[64,256,64]{1,2,0:T(8,128)(2,1)} %broadcast_in_dim.5), calls=%async_computation.3 | async-start | bytes 4194304 | tf_op jit(solution)/shard_map/all_to_all | solution.py:27
Sparse Core Ops, SparseCore 0:
  45.0 303.0 all-gather.1
where the time goes:
time: 495 us; the launch traced here: 494 us
  waiting for transfers between devices  393 us (79%)
  blocking collectives  30.6 us (6%)
  starting transfers between devices  24.3 us (5%)
  local copies, waits for them, and re-layouts  19.8 us (4%)
  between operations  13.5 us (3%)
  matrix products  12.1 us (2%)
    all_gather x1, waiting for transfers between devices, on_device(): pieces = lax.all_gather(stacked, 'mp', axis=2, tiled=True)  303 us
    all_to_all x2, waiting for transfers between devices, copy_for_each(): lax.all_to_all(jnp.broadcast_to(value[None], (length, *value.shape)), axi...  59.2 us
    all_to_all x1, blocking collectives, on_device(): moved = lax.all_to_all(local, 'mp', split_axis=1, concat_axis=1, tiled=True)  30.6 us
    all_to_all x1, waiting for transfers between devices, on_device(): lax.all_to_all(basis, 'mp', split_axis=0, concat_axis=1, tiled=True)  15.7 us
    all_to_all x1, waiting for transfers between devices, summed_on_arrival(): lax.all_to_all(split_up(value, dim, length), axis, 0, 0, tiled=True)  15.2 us
  transfers between devices with their start and end apart: 5, of which 5 were waited for; matrix products, arithmetic and copies ran while one was open for 3% of the time, Pallas kernels for 0%

commit v1 on v0

v1 whole, which is shorter than its diff:
```python
import functools

import jax
import jax.numpy as jnp
from jax import lax
from jax.experimental import pallas as pl
from jax.experimental.pallas import tpu as pltpu
from jax.sharding import Mesh
from jax.sharding import PartitionSpec as P

F32 = jnp.float32
BF16 = jnp.bfloat16
AXES = ("zh", "core", "zl", "xh", "xl", "y")
SIZES = (4, 2, 2, 2, 2, 8)
ROWS = ("zl", "xh")
PLANE = ("zl", "xh", "xl")
COLS = ("xl", "zl", "xh")


def vmem(n):
    return [pl.BlockSpec(memory_space=pltpu.VMEM)] * n


def project_kernel(r_ref, x_ref, y_ref, eig_ref, out_ref, xs, sems):
    steps = eig_ref.shape[0]
    grid_rows = x_ref.shape[1] // (steps * 128)
    r = r_ref[0]

    def copy(s, la):
        src = x_ref if s == 0 else y_ref
        start = pl.multiple_of((la * grid_rows + r) * 128, 128)
        return pltpu.make_async_copy(
            src.at[:, pl.ds(start, 128)], xs.at[s, :, pl.ds(la * 128, 128)], sems.at[s, la]
        )

    for s in range(2):
        for la in range(steps):
            copy(s, la).start()
    lb_n = eig_ref.shape[1]
    basis = jnp.concatenate(
        [eig_ref[:, lb].reshape(steps * 128, 128) for lb in range(lb_n)], 1
    )
    for s in range(2):
        for la in range(steps):
            copy(s, la).wait()
        part = jnp.dot(xs[s], basis, preferred_element_type=F32)
        turned = part.T.astype(BF16)
        out_ref[:, s] = turned.reshape(out_ref.shape[0], out_ref.shape[2], out_ref.shape[3])


def project(r, inputs, upstream, eig):
    tokens = inputs.shape[0]
    steps = eig.shape[0]
    return pl.pallas_call(
        project_kernel,
        out_shape=jax.ShapeDtypeStruct((4, 2, 64, tokens), BF16),
        in_specs=[
            pl.BlockSpec(memory_space=pltpu.SMEM),
            pl.BlockSpec(memory_space=pl.ANY),
            pl.BlockSpec(memory_space=pl.ANY),
            pl.BlockSpec(memory_space=pltpu.VMEM),
        ],
        out_specs=pl.BlockSpec(memory_space=pltpu.VMEM),
        scratch_shapes=[
            pltpu.VMEM((2, tokens, steps * 128), BF16),
            pltpu.SemaphoreType.DMA((2, steps)),
        ],
        name="project",
    )(r, inputs, upstream, eig)


def gram_kernel(core_ref, b_ref, a_ref, keep_ref, send_ref):
    mine = core_ref[0]
    n = a_ref.shape[0] * a_ref.shape[2]
    tokens = a_ref.shape[3]
    half = b_ref.shape[0] // 2
    right_in = a_ref[:, 0].reshape(n, tokens)
    right_up = a_ref[:, 1].reshape(n, tokens)
    over = (((1,), (1,)), ((), ()))
    for out_ref, which in ((send_ref, 1 - mine), (keep_ref, mine)):
        left = b_ref[pl.ds(which * half, half)]
        left_in = left[:, 0].reshape(half * 64, tokens)
        left_up = left[:, 1].reshape(half * 64, tokens)
        block = lax.dot_general(left_in, right_up, over, preferred_element_type=F32)
        block += lax.dot_general(left_up, right_in, over, preferred_element_type=F32)
        out_ref[...] = block.astype(BF16)


def gram_of(core, left, right):
    n = right.shape[0] * right.shape[2]
    shape = jax.ShapeDtypeStruct((left.shape[0] // 2 * 64, n), BF16)
    return pl.pallas_call(
        gram_kernel,
        out_shape=(shape, shape),
        in_specs=[pl.BlockSpec(memory_space=pltpu.SMEM)] + vmem(2),
        out_specs=tuple(vmem(2)),
        name="gram",
    )(core, left, right)


def on_device(inputs, upstream, eig_tiles, eigvals):
    zl, xh, xl, y = (lax.axis_index(a) for a in ("zl", "xh", "xl", "y"))
    zh, core = lax.axis_index("zh"), lax.axis_index("core")
    tokens = inputs.shape[0]
    eig = eig_tiles[0]
    core_at = core.reshape(1).astype(jnp.int32)

    by_b = lax.dynamic_index_in_dim(eigvals.reshape(2, 2, 8, 128), y, 2, keepdims=False)
    lam_b = jnp.transpose(by_b, (1, 0, 2)).reshape(8, 64)
    cube = jnp.transpose(eigvals.reshape(2, 2, 8, 2, 64), (0, 3, 1, 2, 4)).reshape(8, 8, 64)
    lam_a = lax.dynamic_index_in_dim(cube, zl * 4 + xh * 2 + xl, 0, keepdims=False)
    lam_own = lax.dynamic_index_in_dim(lam_a, y, 0, keepdims=False)
    lam_part = lax.dynamic_index_in_dim(lam_b, core * 4 + zh, 0, keepdims=False)

    parts = project((zl * 2 + xh).reshape(1).astype(jnp.int32), inputs, upstream, eig)
    got = lax.all_to_all(parts, ROWS, 0, 0, tiled=True)
    own = jnp.sum(got.astype(F32), 0).astype(BF16)
    copies = jnp.broadcast_to(own[None], (8, *own.shape))
    left = lax.all_to_all(copies, COLS, 0, 0, tiled=True)
    right = lax.all_to_all(copies, "y", 0, 0, tiled=True)
    rows = lax.all_to_all(eig, PLANE, 0, 0, tiled=True)
    basis_rows = jnp.transpose(rows.reshape(4, 2, 2, 128, 128), (0, 3, 1, 2, 4)).reshape(512, 512)

    keep, send = gram_of(core_at, left, right)
    swap = [(0, 1), (1, 0)]
    other = lax.ppermute(send, "core", swap)
    pair = (keep.astype(F32) + other.astype(F32)).astype(BF16).reshape(4, 64, 512)
    share = jnp.sum(lax.all_to_all(pair, "zh", 0, 0, tiled=True).astype(F32), 0)
    s_b = jnp.sqrt(lam_part)[:, None]
    s_a = jnp.sqrt(lam_a.reshape(512))[None, :]
    kernel = -1.0 / (s_b * s_a * (s_b + s_a))
    part = (kernel * (0.5 * share)).astype(BF16)
    mine = lax.all_to_all(jnp.broadcast_to(part[None], (4, 64, 512)), "zh", 0, 0, tiled=True)
    theirs = lax.ppermute(mine, "core", swap)
    first = core == 0
    weighted = jnp.concatenate(
        [jnp.where(first, mine, theirs), jnp.where(first, theirs, mine)], 0
    ).reshape(512, 512)
    proj_in = right[:, 0].reshape(512, tokens)
    mixed_part = jnp.dot(weighted, proj_in, preferred_element_type=F32).astype(BF16)
    mixed = jnp.sum(
        lax.all_to_all(mixed_part.reshape(8, 64, tokens), COLS, 0, 0, tiled=True).astype(F32), 0
    )
    factor = 2.0 / (8 * tokens)
    update = (own[1].astype(F32) / jnp.sqrt(lam_own)[:, None] + factor * mixed).astype(BF16)
    every = lax.all_to_all(jnp.broadcast_to(update[None], (8, 64, tokens)), COLS, 0, 0, tiled=True)
    grad_part = jnp.dot(basis_rows, every.reshape(512, tokens), preferred_element_type=F32)
    blocks = lax.all_to_all(grad_part.astype(BF16).reshape(8, 64, tokens), "y", 0, 0, tiled=True)
    return jnp.sum(blocks.astype(F32), 0).astype(BF16)


def solution(mesh):
    grid = Mesh(mesh.devices.reshape(SIZES), AXES)
    dp, mp = AXES[:2], AXES[2:]
    return jax.shard_map(
        on_device,
        mesh=grid,
        in_specs=(P(dp, None), P(dp, None), P(mp, None, None, None, None), P()),
        out_specs=P(mp, dp),
        check_vma=False,
    )
```

time: 495 us -> 149 us (0.30)
  waiting for transfers between devices: 393 us -> 37.8 us
  blocking collectives: 30.6 us -> 73.2 us
  local copies, waits for them, and re-layouts: 19.8 us -> 3.54 us
  between operations: 13.5 us -> 0.2 us
  matrix products: 12.1 us -> 0.65 us
  Pallas kernels: 0 us -> 6.31 us
    all_gather x1 -> x0, waiting for transfers between devices: 303 us -> none  [on_device(): pieces = lax.all_gather(stacked, 'mp', axis=2, tiled=True)]
    all_to_all x4, waiting for transfers between devices: 90.1 us -> 34.6 us  [the longest x1 10.4 us: on_device(): share = jnp.sum(lax.all_to_all(pair, 'zh', 0, 0, tiled=True).astype(F32), 0)]
    all_to_all x1 -> x5, blocking collectives: 30.6 us -> 73.2 us  [the longest x1 22.5 us: on_device(): right = lax.all_to_all(copies, 'y', 0, 0, tiled=True)]
    dot_general x6 -> x2, matrix products: 12.1 us -> 0.65 us  [the longest x1 0.35 us: on_device(): jnp.dot(basis_rows, every.reshape(512, tokens), preferred_element_type=F32)]
    pallas_call x0 -> x2, Pallas kernels: none -> 6.31 us  [the longest x1 3.94 us: project(): pl.pallas_call(project_kernel, out_shape=jax.ShapeDtypeStruct((4, 2, 64,...]
  transfers between devices with their start and end apart: 5 -> 6, of which waited for: 5 -> 6; matrix products, arithmetic and copies ran while one was open for 3% -> 1% of each run, Pallas kernels for 0% -> 0%
where the time goes in v1:
time: 149 us; the launch traced here: 148 us
  blocking collectives  73.2 us (49%)
  waiting for transfers between devices  37.8 us (25%)
  starting transfers between devices  23.6 us (16%)
  Pallas kernels  6.31 us (4%)
  local copies, waits for them, and re-layouts  3.54 us (2%)
  other arithmetic  2.75 us (2%)
    all_to_all x1, blocking collectives, on_device(): right = lax.all_to_all(copies, 'y', 0, 0, tiled=True)  22.5 us
    all_to_all x1, blocking collectives, on_device(): lax.all_to_all(jnp.broadcast_to(part[None], (4, 64, 512)), 'zh', 0, 0, ti...  13.9 us
    all_to_all x1, blocking collectives, on_device(): got = lax.all_to_all(parts, ROWS, 0, 0, tiled=True)  13.3 us
    all_to_all x1, blocking collectives, on_device(): lax.all_to_all(grad_part.astype(BF16).reshape(8, 64, tokens), 'y', 0, 0,...  12.9 us
    all_to_all x1, blocking collectives, on_device(): lax.all_to_all(mixed_part.reshape(8, 64, tokens), COLS, 0, 0, tiled=True)  10.5 us
    all_to_all x1, waiting for transfers between devices, on_device(): share = jnp.sum(lax.all_to_all(pair, 'zh', 0, 0, tiled=True).astype(F32), 0)  10.4 us
    all_to_all x1, starting transfers between devices, on_device(): share = jnp.sum(lax.all_to_all(pair, 'zh', 0, 0, tiled=True).astype(F32), 0)  9.4 us
    all_to_all x1, waiting for transfers between devices, on_device(): left = lax.all_to_all(copies, COLS, 0, 0, tiled=True)  8.89 us
  transfers between devices with their start and end apart: 6, of which 6 were waited for; matrix products, arithmetic and copies ran while one was open for 1% of the time, Pallas kernels for 0%

profile of v1, /device:TPU:8, one launch (start us, length us, event | category | flops | bytes accessed | tf_op | source)
XLA Modules:
  0.0 148.1 jit_solution(6883132168684748942)
XLA Ops:
  0.0 3.9 %project.1 = bf16[4,2,64,256]{3,2,1,0:T(8,128)(2,1)} custom-call(s32[1]{0:T(128)} %bitcast.r_ref, bf16[256,4096]{1,0:T(8,128)(2,1)} %x_ref.1, bf16[256,4096]{1,0:T(8,128)(2,1)} %y_ref.1, bf16[8,2,128,128]{3,2,1,0:T(8,128)(2,1)} %bitcast.1.eig_ref), custom_call_target="tpu_custom_call" | custom-call | tf_op jit(solution)/shard_map/project/pallas_call | solution.py:54
  3.9 13.3 %all_to_all.45 = bf16[4,2,64,256]{3,2,1,0:T(8,128)(2,1)S(1)} all-to-all(bf16[4,2,64,256]{3,2,1,0:T(8,128)(2,1)} %project.1), channel_id=1, replica_groups=mesh['zh'=4,'core'=2,'zl'=2,'xh'=2,'xl'=2,'y'=8] {'zl','xh'}, dimensions={0} | all-to-all | bytes 524288 | tf_op jit(solution)/shard_map/all_to_all | solution.py:116
  17.3 0.8 broadcast_in_dim.8
  18.2 22.5 %all_to_all.46.a_ref = bf16[8,2,64,256]{3,2,1,0:T(8,128)(2,1)} all-to-all(bf16[8,2,64,256]{3,2,1,0:T(8,128)(2,1)} %broadcast_in_dim.8), channel_id=1, replica_groups=mesh['zh'=4,'core'=2,'zl'=2,'xh'=2,'xl'=2,'y'=8] {'y'}, dimensions={0} | all-to-all | bytes 1048576 | tf_op jit(solution)/shard_map/all_to_all | solution.py:120
  40.7 3.5 %all-to-all-start.1 = ((bf16[8,2,64,256]{3,2,1,0:T(8,128)(2,1)}), bf16[8,2,64,256]{3,2,1,0:T(8,128)(2,1)S(1)}, u32[]{:S(2)}, u32[]{:S(2)}) async-start(bf16[8,2,64,256]{3,2,1,0:T(8,128)(2,1)} %broadcast_in_dim.8), calls=%async_computation.1 | async-start | bytes 1048576 | tf_op jit(solution)/shard_map/all_to_all | solution.py:119
  44.2 8.9 %all-to-all-done.1.b_ref = bf16[8,2,64,256]{3,2,1,0:T(8,128)(2,1)S(1)} async-done(((bf16[8,2,64,256]{3,2,1,0:T(8,128)(2,1)}), bf16[8,2,64,256]{3,2,1,0:T(8,128)(2,1)S(1)}, u32[]{:S(2)}, u32[]{:S(2)}) %all-to-all-start.1) | async-done | bytes 524320 | tf_op jit(solution)/shard_map/all_to_all | solution.py:119
  53.1 0.8 copy-done
  53.9 2.4 %gram.1 = (bf16[256,512]{1,0:T(8,128)(2,1)}, bf16[256,512]{1,0:T(8,128)(2,1)}) custom-call(s32[1]{0:T(128)} %bitcast.9.core_ref, bf16[8,2,64,256]{3,2,1,0:T(8,128)(2,1)} %copy-done, bf16[8,2,64,256]{3,2,1,0:T(8,128)(2,1)} %all_to_all.46.a_ref), custom_call_target="tpu_custom_call" | custom-call | tf_op jit(solution)/shard_map/gram/pallas_call | solution.py:92
  56.2 1.9 %collective-permute-start = (bf16[256,512]{1,0:T(8,128)(2,1)}, bf16[256,512]{1,0:T(8,128)(2,1)S(1)}, u32[]{:S(2)}, u32[]{:S(2)}) collective-permute-start(bf16[256,512]{1,0:T(8,128)(2,1)} %get-tuple-element.8), channel_id=1, source_target_pairs={{0,64},{64,0},{1,65},{65,1},{2,66},{66,2},{3,67},{67,3},{4,68},{68... | collective-permute-start | bytes 786440 | tf_op jit(solution)/shard_map/ppermute | solution.py:126
  58.1 1.7 %collective-permute-done = bf16[256,512]{1,0:T(8,128)(2,1)S(1)} collective-permute-done((bf16[256,512]{1,0:T(8,128)(2,1)}, bf16[256,512]{1,0:T(8,128)(2,1)S(1)}, u32[]{:S(2)}, u32[]{:S(2)}) %collective-permute-start) | collective-permute-done | bytes 262176 | tf_op jit(solution)/shard_map/ppermute | solution.py:126
  59.9 1.7 %add_convert_fusion = bf16[256,512]{1,0:T(8,128)(2,1)} fusion(bf16[256,512]{1,0:T(8,128)(2,1)S(1)} %collective-permute-done, bf16[256,512]{1,0:T(8,128)(2,1)} %get-tuple-element.7), kind=kLoop, calls=%fused_computation.7 | loop fusion | flops 524288 | bytes 786432 | tf_op jit(solution)/shard_map/convert_element_type | solution.py:127
  61.6 9.4 %all-to-all-start.3 = ((bf16[4,64,512]{2,1,0:T(8,128)(2,1)}), bf16[4,64,512]{2,1,0:T(8,128)(2,1)S(1)}, u32[]{:S(2)}, u32[]{:S(2)}) async-start(bf16[4,64,512]{2,1,0:T(8,128)(2,1)} %bitcast.10), calls=%async_computation.3 | async-start | bytes 524288 | tf_op jit(solution)/shard_map/all_to_all | solution.py:128
  71.3 10.4 %all-to-all-done.3 = bf16[4,64,512]{2,1,0:T(8,128)(2,1)S(1)} async-done(((bf16[4,64,512]{2,1,0:T(8,128)(2,1)}), bf16[4,64,512]{2,1,0:T(8,128)(2,1)S(1)}, u32[]{:S(2)}, u32[]{:S(2)}) %all-to-all-start.3) | async-done | bytes 262176 | tf_op jit(solution)/shard_map/all_to_all | solution.py:128
  81.9 13.9 %all_to_all.47 = bf16[4,64,512]{2,1,0:T(8,128)(2,1)S(1)} all-to-all(bf16[4,64,512]{2,1,0:T(8,128)(2,1)S(1)} %broadcast_in_dim.9), channel_id=1, replica_groups=mesh['zh'=4,'core'=2,'zl'=2,'xh'=2,'xl'=2,'y'=8] {'zh'}, dimensions={0} | all-to-all | bytes 524288 | tf_op jit(solution)/shard_map/all_to_all | solution.py:133
  95.8 1.9 %collective-permute-start.1 = (bf16[4,64,512]{2,1,0:T(8,128)(2,1)S(1)}, bf16[4,64,512]{2,1,0:T(8,128)(2,1)S(1)}, u32[]{:S(2)}, u32[]{:S(2)}) collective-permute-start(bf16[4,64,512]{2,1,0:T(8,128)(2,1)S(1)} %all_to_all.47), channel_id=1, source_target_pairs={{0,64},{64,0},{1,65},{65,1},{2,66},{66,2},{3,67},{67,3},{4,68},{68... | collective-permute-start | bytes 786440 | tf_op jit(solution)/shard_map/ppermute | solution.py:134
  97.7 1.5 %collective-permute-done.1 = bf16[4,64,512]{2,1,0:T(8,128)(2,1)S(1)} collective-permute-done((bf16[4,64,512]{2,1,0:T(8,128)(2,1)S(1)}, bf16[4,64,512]{2,1,0:T(8,128)(2,1)S(1)}, u32[]{:S(2)}, u32[]{:S(2)}) %collective-permute-start.1) | collective-permute-done | bytes 262176 | tf_op jit(solution)/shard_map/ppermute | solution.py:134
  99.6 10.5 %all_to_all.48 = bf16[8,64,256]{2,1,0:T(8,128)(2,1)S(1)} all-to-all(bf16[8,64,256]{2,1,0:T(8,128)(2,1)S(1)} %bitcast.43), channel_id=1, replica_groups=mesh['zh'=4,'core'=2,'zl'=2,'xh'=2,'xl'=2,'y'=8] {'xl','zl','xh'}, dimensions={0} | all-to-all | bytes 524288 | tf_op jit(solution)/shard_map/all_to_all | solution.py:142
  110.2 3.5 %all-to-all-start.7 = ((bf16[8,2,128,128]{3,2,1,0:T(8,128)(2,1)}), bf16[8,2,128,128]{3,2,1,0:T(8,128)(2,1)S(1)}, u32[]{:S(2)}, u32[]{:S(2)}) async-start(bf16[8,2,128,128]{3,2,1,0:T(8,128)(2,1)} %bitcast.1.eig_ref), calls=%async_computation.7 | async-start | bytes 1048576 | tf_op jit(solution)/shard_map/all_to_all | solution.py:121
  113.8 8.6 %all-to-all-done.7 = bf16[8,2,128,128]{3,2,1,0:T(8,128)(2,1)S(1)} async-done(((bf16[8,2,128,128]{3,2,1,0:T(8,128)(2,1)}), bf16[8,2,128,128]{3,2,1,0:T(8,128)(2,1)S(1)}, u32[]{:S(2)}, u32[]{:S(2)}) %all-to-all-start.7) | async-done | bytes 524320 | tf_op jit(solution)/shard_map/all_to_all | solution.py:121
  122.4 0.7 broadcast_in_dim.11
  123.1 3.4 %all-to-all-start.6 = ((bf16[8,64,256]{2,1,0:T(8,128)(2,1)}), bf16[8,64,256]{2,1,0:T(8,128)(2,1)S(1)}, u32[]{:S(2)}, u32[]{:S(2)}) async-start(bf16[8,64,256]{2,1,0:T(8,128)(2,1)} %broadcast_in_dim.11), calls=%async_computation.6 | async-start | bytes 524288 | tf_op jit(solution)/shard_map/all_to_all | solution.py:146
  127.3 6.7 %all-to-all-done.6 = bf16[8,64,256]{2,1,0:T(8,128)(2,1)S(1)} async-done(((bf16[8,64,256]{2,1,0:T(8,128)(2,1)}), bf16[8,64,256]{2,1,0:T(8,128)(2,1)S(1)}, u32[]{:S(2)}, u32[]{:S(2)}) %all-to-all-start.6) | async-done | bytes 262176 | tf_op jit(solution)/shard_map/all_to_all | solution.py:146
  134.5 12.9 %all_to_all.49 = bf16[8,64,256]{2,1,0:T(8,128)(2,1)S(1)} all-to-all(bf16[8,64,256]{2,1,0:T(8,128)(2,1)S(1)} %bitcast.41), channel_id=1, replica_groups=mesh['zh'=4,'core'=2,'zl'=2,'xh'=2,'xl'=2,'y'=8] {'y'}, dimensions={0} | all-to-all | bytes 524288 | tf_op jit(solution)/shard_map/all_to_all | solution.py:148
  147.4 0.7 reduce_sum.45
  (27 shorter events, 2.2 us)
Async XLA Ops:
  18.2 52.8 %copy-start.1 = (f32[4096]{0:T(1024)S(1)}, f32[4096]{0:T(1024)}, u32[]{:S(2)}) copy-start(f32[4096]{0:T(1024)} %param.7) | copy-start | bytes 49156
  40.7 12.4 %all-to-all-start.1 = ((bf16[8,2,64,256]{3,2,1,0:T(8,128)(2,1)}), bf16[8,2,64,256]{3,2,1,0:T(8,128)(2,1)S(1)}, u32[]{:S(2)}, u32[]{:S(2)}) async-start(bf16[8,2,64,256]{3,2,1,0:T(8,128)(2,1)} %broadcast_in_dim.8), calls=%async_computation.1 | async-start | bytes 1048576 | tf_op jit(solution)/shard_map/all_to_all | solution.py:119
  53.1 0.8 copy-start
  56.2 3.6 %collective-permute-start = (bf16[256,512]{1,0:T(8,128)(2,1)}, bf16[256,512]{1,0:T(8,128)(2,1)S(1)}, u32[]{:S(2)}, u32[]{:S(2)}) collective-permute-start(bf16[256,512]{1,0:T(8,128)(2,1)} %get-tuple-element.8), channel_id=1, source_target_pairs={{0,64},{64,0},{1,65},{65,1},{2,66},{66,2},{3,67},{67,3},{4,68},{68... | collective-permute-start | bytes 786440 | tf_op jit(solution)/shard_map/ppermute | solution.py:126
  61.6 20.1 %all-to-all-start.3 = ((bf16[4,64,512]{2,1,0:T(8,128)(2,1)}), bf16[4,64,512]{2,1,0:T(8,128)(2,1)S(1)}, u32[]{:S(2)}, u32[]{:S(2)}) async-start(bf16[4,64,512]{2,1,0:T(8,128)(2,1)} %bitcast.10), calls=%async_computation.3 | async-start | bytes 524288 | tf_op jit(solution)/shard_map/all_to_all | solution.py:128
  71.1 28.2 %slice-start = ((bf16[8,2,64,256]{3,2,1,0:T(8,128)(2,1)}), bf16[8,1,64,256]{3,2,1,0:T(8,128)(2,1)S(1)}, s32[]{:S(2)}) async-start(bf16[8,2,64,256]{3,2,1,0:T(8,128)(2,1)} %all_to_all.46.a_ref), calls=%async_computation.9 | async-start | bytes 524288 | tf_op jit(solution)/shard_map/slice | solution.py:139
  95.8 3.4 %collective-permute-start.1 = (bf16[4,64,512]{2,1,0:T(8,128)(2,1)S(1)}, bf16[4,64,512]{2,1,0:T(8,128)(2,1)S(1)}, u32[]{:S(2)}, u32[]{:S(2)}) collective-permute-start(bf16[4,64,512]{2,1,0:T(8,128)(2,1)S(1)} %all_to_all.47), channel_id=1, source_target_pairs={{0,64},{64,0},{1,65},{65,1},{2,66},{66,2},{3,67},{67,3},{4,68},{68... | collective-permute-start | bytes 786440 | tf_op jit(solution)/shard_map/ppermute | solution.py:134
  110.2 12.2 %all-to-all-start.7 = ((bf16[8,2,128,128]{3,2,1,0:T(8,128)(2,1)}), bf16[8,2,128,128]{3,2,1,0:T(8,128)(2,1)S(1)}, u32[]{:S(2)}, u32[]{:S(2)}) async-start(bf16[8,2,128,128]{3,2,1,0:T(8,128)(2,1)} %bitcast.1.eig_ref), calls=%async_computation.7 | async-start | bytes 1048576 | tf_op jit(solution)/shard_map/all_to_all | solution.py:121
  123.1 10.9 %all-to-all-start.6 = ((bf16[8,64,256]{2,1,0:T(8,128)(2,1)}), bf16[8,64,256]{2,1,0:T(8,128)(2,1)S(1)}, u32[]{:S(2)}, u32[]{:S(2)}) async-start(bf16[8,64,256]{2,1,0:T(8,128)(2,1)} %broadcast_in_dim.11), calls=%async_computation.6 | async-start | bytes 524288 | tf_op jit(solution)/shard_map/all_to_all | solution.py:146

commit v2 on v1

--- a/solution.py
+++ b/solution.py
@@ -1,5 +1,3 @@
-import functools
-
 import jax
 import jax.numpy as jnp
 from jax import lax
@@ -21,7 +19,8 @@
     return [pl.BlockSpec(memory_space=pltpu.VMEM)] * n
 
 
-def project_kernel(r_ref, x_ref, y_ref, eig_ref, out_ref, xs, sems):
+def project_kernel(r_ref, x_ref, y_ref, eig_ref, *refs):
+    *out_refs, blocks, xs, sems = refs
     steps = eig_ref.shape[0]
     grid_rows = x_ref.shape[1] // (steps * 128)
     r = r_ref[0]
@@ -44,8 +43,9 @@
         for la in range(steps):
             copy(s, la).wait()
         part = jnp.dot(xs[s], basis, preferred_element_type=F32)
-        turned = part.T.astype(BF16)
-        out_ref[:, s] = turned.reshape(out_ref.shape[0], out_ref.shape[2], out_ref.shape[3])
+        blocks[:, s] = part.T.astype(BF16).reshape(blocks.shape[0], *blocks.shape[2:])
+    for k, out_ref in enumerate(out_refs):
+        out_ref[...] = blocks[r ^ k]
 
 
 def project(r, inputs, upstream, eig):
@@ -53,15 +53,16 @@
     steps = eig.shape[0]
     return pl.pallas_call(
         project_kernel,
-        out_shape=jax.ShapeDtypeStruct((4, 2, 64, tokens), BF16),
+        out_shape=(jax.ShapeDtypeStruct((2, 64, tokens), BF16),) * 4,
         in_specs=[
             pl.BlockSpec(memory_space=pltpu.SMEM),
             pl.BlockSpec(memory_space=pl.ANY),
             pl.BlockSpec(memory_space=pl.ANY),
             pl.BlockSpec(memory_space=pltpu.VMEM),
         ],
-        out_specs=pl.BlockSpec(memory_space=pltpu.VMEM),
+        out_specs=tuple(vmem(4)),
         scratch_shapes=[
+            pltpu.VMEM((4, 2, 64, tokens), BF16),
             pltpu.VMEM((2, tokens, steps * 128), BF16),
             pltpu.SemaphoreType.DMA((2, steps)),
         ],
@@ -69,33 +70,63 @@
     )(r, inputs, upstream, eig)
 
 
-def gram_kernel(core_ref, b_ref, a_ref, keep_ref, send_ref):
-    mine = core_ref[0]
+def spread_kernel(*refs):
+    *parts, _, own_ref, copies_ref = refs
+    total = parts[0][...].astype(F32)
+    for part in parts[1:]:
+        total += part[...].astype(F32)
+    own = total.astype(BF16)
+    own_ref[...] = own
+    for k in range(copies_ref.shape[0]):
+        copies_ref[k] = own
+
+
+def spread(parts, after):
+    shape = parts[0].shape
+    return pl.pallas_call(
+        spread_kernel,
+        out_shape=(
+            jax.ShapeDtypeStruct(shape, BF16),
+            jax.ShapeDtypeStruct((8, *shape), BF16),
+        ),
+        in_specs=vmem(len(parts)) + [pl.BlockSpec(memory_space=pl.ANY)],
+        out_specs=tuple(vmem(2)),
+        name="spread",
+    )(*parts, after)
+
+
+def gram_kernel(at_ref, own_ref, one_ref, two_ref, four_ref, a_ref, keep_ref, send_ref, left):
+    mine, here = at_ref[0], at_ref[1]
     n = a_ref.shape[0] * a_ref.shape[2]
     tokens = a_ref.shape[3]
-    half = b_ref.shape[0] // 2
+    half = left.shape[0] // 2
+    pieces = [own_ref, one_ref] + [two_ref.at[i] for i in range(2)]
+    pieces += [four_ref.at[i] for i in range(4)]
+    for k, piece in enumerate(pieces):
+        left[here ^ ((k & 1) * 4 + (k >> 1))] = piece[...]
     right_in = a_ref[:, 0].reshape(n, tokens)
     right_up = a_ref[:, 1].reshape(n, tokens)
     over = (((1,), (1,)), ((), ()))
     for out_ref, which in ((send_ref, 1 - mine), (keep_ref, mine)):
-        left = b_ref[pl.ds(which * half, half)]
-        left_in = left[:, 0].reshape(half * 64, tokens)
-        left_up = left[:, 1].reshape(half * 64, tokens)
+        rows = left[pl.ds(which * half, half)]
+        left_in = rows[:, 0].reshape(half * 64, tokens)
+        left_up = rows[:, 1].reshape(half * 64, tokens)
         block = lax.dot_general(left_in, right_up, over, preferred_element_type=F32)
         block += lax.dot_general(left_up, right_in, over, preferred_element_type=F32)
         out_ref[...] = block.astype(BF16)
 
 
-def gram_of(core, left, right):
+def gram_of(at, pieces, right):
     n = right.shape[0] * right.shape[2]
-    shape = jax.ShapeDtypeStruct((left.shape[0] // 2 * 64, n), BF16)
+    shape = jax.ShapeDtypeStruct((4 * 64, n), BF16)
     return pl.pallas_call(
         gram_kernel,
         out_shape=(shape, shape),
-        in_specs=[pl.BlockSpec(memory_space=pltpu.SMEM)] + vmem(2),
+        in_specs=[pl.BlockSpec(memory_space=pltpu.SMEM)] + vmem(5),
         out_specs=tuple(vmem(2)),
+        scratch_shapes=[pltpu.VMEM(right.shape, BF16)],
         name="gram",
-    )(core, left, right)
+    )(at, *pieces, right)
 
 
 def on_device(inputs, upstream, eig_tiles, eigvals):
@@ -103,7 +134,6 @@
     zh, core = lax.axis_index("zh"), lax.axis_index("core")
     tokens = inputs.shape[0]
     eig = eig_tiles[0]
-    core_at = core.reshape(1).astype(jnp.int32)
 
     by_b = lax.dynamic_index_in_dim(eigvals.reshape(2, 2, 8, 128), y, 2, keepdims=False)
     lam_b = jnp.transpose(by_b, (1, 0, 2)).reshape(8, 64)
@@ -112,17 +142,23 @@
     lam_own = lax.dynamic_index_in_dim(lam_a, y, 0, keepdims=False)
     lam_part = lax.dynamic_index_in_dim(lam_b, core * 4 + zh, 0, keepdims=False)
 
-    parts = project((zl * 2 + xh).reshape(1).astype(jnp.int32), inputs, upstream, eig)
-    got = lax.all_to_all(parts, ROWS, 0, 0, tiled=True)
-    own = jnp.sum(got.astype(F32), 0).astype(BF16)
-    copies = jnp.broadcast_to(own[None], (8, *own.shape))
-    left = lax.all_to_all(copies, COLS, 0, 0, tiled=True)
+    rows = lax.all_to_all(eig, PLANE, 0, 0, tiled=True)
+    r = zl * 2 + xh
+    parts = project(r.reshape(1).astype(jnp.int32), inputs, upstream, eig)
+    got = [parts[0]]
+    for k in range(1, 4):
+        got.append(lax.ppermute(parts[k], ROWS, [(i, i ^ k) for i in range(4)]))
+    own, copies = spread(got, rows)
     right = lax.all_to_all(copies, "y", 0, 0, tiled=True)
-    rows = lax.all_to_all(eig, PLANE, 0, 0, tiled=True)
+    swap = [(0, 1), (1, 0)]
+    one = lax.ppermute(own, "xl", swap)
+    pair_of = jnp.stack([own, one])
+    two = lax.ppermute(pair_of, "xh", swap)
+    four = lax.ppermute(jnp.concatenate([pair_of, two]), "zl", swap)
     basis_rows = jnp.transpose(rows.reshape(4, 2, 2, 128, 128), (0, 3, 1, 2, 4)).reshape(512, 512)
 
-    keep, send = gram_of(core_at, left, right)
-    swap = [(0, 1), (1, 0)]
+    at = jnp.stack([core, xl * 4 + r]).astype(jnp.int32)
+    keep, send = gram_of(at, (own, one, two, four), right)
     other = lax.ppermute(send, "core", swap)
     pair = (keep.astype(F32) + other.astype(F32)).astype(BF16).reshape(4, 64, 512)
     share = jnp.sum(lax.all_to_all(pair, "zh", 0, 0, tiled=True).astype(F32), 0)

time: 149 us -> 153 us (1.027)
  blocking collectives: 73.2 us -> 30 us
  starting transfers between devices: 23.6 us -> 52 us
  waiting for transfers between devices: 37.8 us -> 50.1 us
  other arithmetic: 2.75 us -> 5.14 us
  Pallas kernels: 6.31 us -> 8.23 us
    all_to_all x3 -> x0, blocking collectives: 46.4 us -> none  [the longest x1 22.5 us: on_device(): right = lax.all_to_all(copies, 'y', 0, 0, tiled=True)]
    ppermute x0 -> x6, waiting for transfers between devices: none -> 21.7 us  [the longest x3 6.82 us: on_device(): got.append(lax.ppermute(parts[k], ROWS, [(i, i ^ k) for i in range(4)]))]
    ppermute x0 -> x6, starting transfers between devices: none -> 18.2 us  [the longest x3 10.7 us: on_device(): got.append(lax.ppermute(parts[k], ROWS, [(i, i ^ k) for i in range(4)]))]
    all_to_all x1, waiting for transfers between devices: 8.58 us -> 0.01 us  [on_device(): rows = lax.all_to_all(eig, PLANE, 0, 0, tiled=True)]
    all_to_all x1 -> x2, starting transfers between devices: 3.49 us -> 11.1 us  [the longest x1 7.68 us: on_device(): right = lax.all_to_all(copies, 'y', 0, 0, tiled=True)]
    all_to_all x1, blocking collectives: 12.9 us -> 16 us  [on_device(): lax.all_to_all(grad_part.astype(BF16).reshape(8, 64, tokens), 'y', 0, 0,...]
    all_to_all x1, starting transfers between devices: 3.5 us -> 6.11 us  [on_device(): rows = lax.all_to_all(eig, PLANE, 0, 0, tiled=True)]
    pallas_call x1 -> x2, Pallas kernels: 3.94 us -> 5.79 us  [the longest x1 3.98 us: project(): pl.pallas_call(project_kernel, out_shape=(jax.ShapeDtypeStruct((2, 64, to...]
  transfers between devices with their start and end apart: 6 -> 13, of which waited for: 6 -> 10; matrix products, arithmetic and copies ran while one was open for 1% -> 2% of each run, Pallas kernels for 0% -> 3%
where the time goes in v2:
time: 153 us; the launch traced here: 151 us
  starting transfers between devices  52 us (34%)
  waiting for transfers between devices  50.1 us (33%)
  blocking collectives  30 us (20%)
  Pallas kernels  8.23 us (5%)
  other arithmetic  5.14 us (3%)
  local copies, waits for them, and re-layouts  4.22 us (3%)
    all_to_all x1, blocking collectives, on_device(): lax.all_to_all(grad_part.astype(BF16).reshape(8, 64, tokens), 'y', 0, 0,...  16 us
    all_to_all x1, blocking collectives, on_device(): lax.all_to_all(jnp.broadcast_to(part[None], (4, 64, 512)), 'zh', 0, 0, ti...  13.9 us
    ppermute x3, starting transfers between devices, on_device(): got.append(lax.ppermute(parts[k], ROWS, [(i, i ^ k) for i in range(4)]))  10.7 us
    all_to_all x1, waiting for transfers between devices, on_device(): share = jnp.sum(lax.all_to_all(pair, 'zh', 0, 0, tiled=True).astype(F32), 0)  10.4 us
    all_to_all x1, starting transfers between devices, on_device(): share = jnp.sum(lax.all_to_all(pair, 'zh', 0, 0, tiled=True).astype(F32), 0)  9.4 us
    all_to_all x1, waiting for transfers between devices, on_device(): lax.all_to_all(mixed_part.reshape(8, 64, tokens), COLS, 0, 0, tiled=True)  8.02 us
    all_to_all x1, starting transfers between devices, on_device(): right = lax.all_to_all(copies, 'y', 0, 0, tiled=True)  7.68 us
    ppermute x3, waiting for transfers between devices, on_device(): got.append(lax.ppermute(parts[k], ROWS, [(i, i ^ k) for i in range(4)]))  6.82 us
  transfers between devices with their start and end apart: 13, of which 10 were waited for; matrix products, arithmetic and copies ran while one was open for 2% of the time, Pallas kernels for 3%

profile of v2, /device:TPU:8, one launch (start us, length us, event | category | flops | bytes accessed | tf_op | source)
XLA Modules:
  0.0 151.3 jit_solution(13738127405777187557)
XLA Ops:
  0.0 6.1 %all-to-all-start = ((bf16[8,2,128,128]{3,2,1,0:T(8,128)(2,1)}), bf16[8,2,128,128]{3,2,1,0:T(8,128)(2,1)S(1)}, u32[]{:S(2)}, u32[]{:S(2)}) async-start(bf16[8,2,128,128]{3,2,1,0:T(8,128)(2,1)} %bitcast.42), calls=%async_computation | async-start | bytes 1048576 | tf_op jit(solution)/shard_map/all_to_all | solution.py:145
  6.1 4.0 %project.1 = (bf16[2,64,256]{2,1,0:T(8,128)(2,1)}, bf16[2,64,256]{2,1,0:T(8,128)(2,1)}, bf16[2,64,256]{2,1,0:T(8,128)(2,1)}, bf16[2,64,256]{2,1,0:T(8,128)(2,1)}) custom-call(s32[1]{0:T(128)} %bitcast.r_ref, bf16[256,4096]{1,0:T(8,128)(2,1)} %x_ref.1, bf16[256,4096]{1,0:T(8,128)(2,1)} %y_ref.1, bf16[8,2,128,128]{3,2,1,0:T(8,128)(2,1)} %bitcast.43), custom_call_target="tpu_custom_call" | custom-call | tf_op jit(solution)/shard_map/project/pallas_call | solution.py:54
  10.1 5.4 %collective-permute-start = (bf16[2,64,256]{2,1,0:T(8,128)(2,1)}, bf16[2,64,256]{2,1,0:T(8,128)(2,1)S(1)}, u32[]{:S(2)}, u32[]{:S(2)}) collective-permute-start(bf16[2,64,256]{2,1,0:T(8,128)(2,1)} %get-tuple-element.14), channel_id=1, source_target_pairs={{0,16},{16,0},{32,48},{48,32},{1,17},{17,1},{33,49},{49,33},{2,18}... | collective-permute-start | bytes 196616 | tf_op jit(solution)/shard_map/ppermute | solution.py:150
  15.5 3.4 %collective-permute-start.1 = (bf16[2,64,256]{2,1,0:T(8,128)(2,1)}, bf16[2,64,256]{2,1,0:T(8,128)(2,1)S(1)}, u32[]{:S(2)}, u32[]{:S(2)}) collective-permute-start(bf16[2,64,256]{2,1,0:T(8,128)(2,1)} %get-tuple-element.15), channel_id=1, source_target_pairs={{0,32},{16,48},{32,0},{48,16},{1,33},{17,49},{33,1},{49,17},{2,34}... | collective-permute-start | bytes 196616 | tf_op jit(solution)/shard_map/ppermute | solution.py:150
  18.9 1.9 %collective-permute-start.2 = (bf16[2,64,256]{2,1,0:T(8,128)(2,1)}, bf16[2,64,256]{2,1,0:T(8,128)(2,1)S(1)}, u32[]{:S(2)}, u32[]{:S(2)}) collective-permute-start(bf16[2,64,256]{2,1,0:T(8,128)(2,1)} %get-tuple-element.16), channel_id=1, source_target_pairs={{0,48},{16,32},{32,16},{48,0},{1,49},{17,33},{33,17},{49,1},{2,50}... | collective-permute-start | bytes 196616 | tf_op jit(solution)/shard_map/ppermute | solution.py:150
  21.9 5.8 %collective-permute-done.2.refs_3_ = bf16[2,64,256]{2,1,0:T(8,128)(2,1)S(1)} collective-permute-done((bf16[2,64,256]{2,1,0:T(8,128)(2,1)}, bf16[2,64,256]{2,1,0:T(8,128)(2,1)S(1)}, u32[]{:S(2)}, u32[]{:S(2)}) %collective-permute-start.2) | collective-permute-done | bytes 65568 | tf_op jit(solution)/shard_map/ppermute | solution.py:150
  30.3 7.7 %all-to-all-start.1 = ((bf16[8,2,64,256]{3,2,1,0:T(8,128)(2,1)}), bf16[8,2,64,256]{3,2,1,0:T(8,128)(2,1)S(1)}, u32[]{:S(2)}, u32[]{:S(2)}) async-start(bf16[8,2,64,256]{3,2,1,0:T(8,128)(2,1)} %get-tuple-element.18), calls=%async_computation.1 | async-start | bytes 1048576 | tf_op jit(solution)/shard_map/all_to_all | solution.py:152
  38.0 2.5 %collective-permute-start.3 = (bf16[2,64,256]{2,1,0:T(8,128)(2,1)}, bf16[2,64,256]{2,1,0:T(8,128)(2,1)S(1)}, u32[]{:S(2)}, u32[]{:S(2)}) collective-permute-start(bf16[2,64,256]{2,1,0:T(8,128)(2,1)} %get-tuple-element.17.own_ref), channel_id=1, source_target_pairs={{0,8},{8,0},{1,9},{9,1},{2,10},{10,2},{3,11},{11,3},{4,12},{12,4},... | collective-permute-start | bytes 196616 | tf_op jit(solution)/shard_map/ppermute | solution.py:154
  40.5 3.9 %collective-permute-done.3.one_ref = bf16[2,64,256]{2,1,0:T(8,128)(2,1)S(1)} collective-permute-done((bf16[2,64,256]{2,1,0:T(8,128)(2,1)}, bf16[2,64,256]{2,1,0:T(8,128)(2,1)S(1)}, u32[]{:S(2)}, u32[]{:S(2)}) %collective-permute-start.3) | collective-permute-done | bytes 65568 | tf_op jit(solution)/shard_map/ppermute | solution.py:154
  45.3 2.5 %collective-permute-start.4 = (bf16[2,2,64,256]{3,2,1,0:T(8,128)(2,1)S(1)}, bf16[2,2,64,256]{3,2,1,0:T(8,128)(2,1)S(1)}, u32[]{:S(2)}, u32[]{:S(2)}) collective-permute-start(bf16[2,2,64,256]{3,2,1,0:T(8,128)(2,1)S(1)} %pad_maximum_fusion.2), channel_id=1, source_target_pairs={{0,16},{16,0},{1,17},{17,1},{2,18},{18,2},{3,19},{19,3},{4,20},{20... | collective-permute-start | bytes 393224 | tf_op jit(solution)/shard_map/ppermute | solution.py:156
  47.8 5.8 %collective-permute-done.4.two_ref = bf16[2,2,64,256]{3,2,1,0:T(8,128)(2,1)S(1)} collective-permute-done((bf16[2,2,64,256]{3,2,1,0:T(8,128)(2,1)S(1)}, bf16[2,2,64,256]{3,2,1,0:T(8,128)(2,1)S(1)}, u32[]{:S(2)}, u32[]{:S(2)}) %collective-permute-start.4) | collective-permute-done | bytes 131104 | tf_op jit(solution)/shard_map/ppermute | solution.py:156
  54.5 2.5 %collective-permute-start.5 = (bf16[4,2,64,256]{3,2,1,0:T(8,128)(2,1)S(1)}, bf16[4,2,64,256]{3,2,1,0:T(8,128)(2,1)S(1)}, u32[]{:S(2)}, u32[]{:S(2)}) collective-permute-start(bf16[4,2,64,256]{3,2,1,0:T(8,128)(2,1)S(1)} %pad_maximum_fusion.1), channel_id=1, source_target_pairs={{0,32},{32,0},{1,33},{33,1},{2,34},{34,2},{3,35},{35,3},{4,36},{36... | collective-permute-start | bytes 786440 | tf_op jit(solution)/shard_map/ppermute | solution.py:157
  57.6 5.2 %collective-permute-done.5.four_ref = bf16[4,2,64,256]{3,2,1,0:T(8,128)(2,1)S(1)} collective-permute-done((bf16[4,2,64,256]{3,2,1,0:T(8,128)(2,1)S(1)}, bf16[4,2,64,256]{3,2,1,0:T(8,128)(2,1)S(1)}, u32[]{:S(2)}, u32[]{:S(2)}) %collective-permute-start.5) | collective-permute-done | bytes 262176 | tf_op jit(solution)/shard_map/ppermute | solution.py:157
  64.3 2.4 %gram.1 = (bf16[256,512]{1,0:T(8,128)(2,1)}, bf16[256,512]{1,0:T(8,128)(2,1)}) custom-call(s32[2]{0:T(128)} %pad_add_fusion.at_ref, bf16[2,64,256]{2,1,0:T(8,128)(2,1)} %get-tuple-element.17.own_ref, bf16[2,64,256]{2,1,0:T(8,128)(2,1)} %copy-done.4, bf16[2,2,64,256]{3,2,1,0:T(8,128)(2,1)} %copy-done.5, bf16[4,2,64,256]{3,2,1,0:T(8,128)(2,1)} %copy-done.6, ...), custom_call_target="tpu_custom_call" | custom-call | tf_op jit(solution)/shard_map/gram/pallas_call | solution.py:122
  66.8 1.9 %collective-permute-start.6 = (bf16[256,512]{1,0:T(8,128)(2,1)}, bf16[256,512]{1,0:T(8,128)(2,1)S(1)}, u32[]{:S(2)}, u32[]{:S(2)}) collective-permute-start(bf16[256,512]{1,0:T(8,128)(2,1)} %get-tuple-element.20), channel_id=1, source_target_pairs={{0,64},{64,0},{1,65},{65,1},{2,66},{66,2},{3,67},{67,3},{4,68},{68... | collective-permute-start | bytes 786440 | tf_op jit(solution)/shard_map/ppermute | solution.py:162
  72.1 9.4 %all-to-all-start.2 = ((bf16[4,64,512]{2,1,0:T(8,128)(2,1)}), bf16[4,64,512]{2,1,0:T(8,128)(2,1)S(1)}, u32[]{:S(2)}, u32[]{:S(2)}) async-start(bf16[4,64,512]{2,1,0:T(8,128)(2,1)} %bitcast.13), calls=%async_computation.2 | async-start | bytes 524288 | tf_op jit(solution)/shard_map/all_to_all | solution.py:164
  81.8 10.4 %all-to-all-done.2 = bf16[4,64,512]{2,1,0:T(8,128)(2,1)S(1)} async-done(((bf16[4,64,512]{2,1,0:T(8,128)(2,1)}), bf16[4,64,512]{2,1,0:T(8,128)(2,1)S(1)}, u32[]{:S(2)}, u32[]{:S(2)}) %all-to-all-start.2) | async-done | bytes 262176 | tf_op jit(solution)/shard_map/all_to_all | solution.py:164
  92.4 13.9 %all_to_all.35 = bf16[4,64,512]{2,1,0:T(8,128)(2,1)S(1)} all-to-all(bf16[4,64,512]{2,1,0:T(8,128)(2,1)S(1)} %broadcast_in_dim.6), channel_id=1, replica_groups=mesh['zh'=4,'core'=2,'zl'=2,'xh'=2,'xl'=2,'y'=8] {'zh'}, dimensions={0} | all-to-all | bytes 524288 | tf_op jit(solution)/shard_map/all_to_all | solution.py:169
  106.4 1.9 %collective-permute-start.7 = (bf16[4,64,512]{2,1,0:T(8,128)(2,1)S(1)}, bf16[4,64,512]{2,1,0:T(8,128)(2,1)S(1)}, u32[]{:S(2)}, u32[]{:S(2)}) collective-permute-start(bf16[4,64,512]{2,1,0:T(8,128)(2,1)S(1)} %all_to_all.35), channel_id=1, source_target_pairs={{0,64},{64,0},{1,65},{65,1},{2,66},{66,2},{3,67},{67,3},{4,68},{68... | collective-permute-start | bytes 786440 | tf_op jit(solution)/shard_map/ppermute | solution.py:170
  110.9 3.4 %all-to-all-start.4 = ((bf16[8,64,256]{2,1,0:T(8,128)(2,1)}), bf16[8,64,256]{2,1,0:T(8,128)(2,1)S(1)}, u32[]{:S(2)}, u32[]{:S(2)}) async-start(bf16[8,64,256]{2,1,0:T(8,128)(2,1)} %bitcast.16), calls=%async_computation.4 | async-start | bytes 524288 | tf_op jit(solution)/shard_map/all_to_all | solution.py:178
  114.4 8.0 %all-to-all-done.4 = bf16[8,64,256]{2,1,0:T(8,128)(2,1)S(1)} async-done(((bf16[8,64,256]{2,1,0:T(8,128)(2,1)}), bf16[8,64,256]{2,1,0:T(8,128)(2,1)S(1)}, u32[]{:S(2)}, u32[]{:S(2)}) %all-to-all-start.4) | async-done | bytes 262176 | tf_op jit(solution)/shard_map/all_to_all | solution.py:178
  123.2 3.4 %all-to-all-start.5 = ((bf16[8,64,256]{2,1,0:T(8,128)(2,1)}), bf16[8,64,256]{2,1,0:T(8,128)(2,1)S(1)}, u32[]{:S(2)}, u32[]{:S(2)}) async-start(bf16[8,64,256]{2,1,0:T(8,128)(2,1)} %broadcast_in_dim.8), calls=%async_computation.5 | async-start | bytes 524288 | tf_op jit(solution)/shard_map/all_to_all | solution.py:182
  127.4 6.7 %all-to-all-done.5 = bf16[8,64,256]{2,1,0:T(8,128)(2,1)S(1)} async-done(((bf16[8,64,256]{2,1,0:T(8,128)(2,1)}), bf16[8,64,256]{2,1,0:T(8,128)(2,1)S(1)}, u32[]{:S(2)}, u32[]{:S(2)}) %all-to-all-start.5) | async-done | bytes 262176 | tf_op jit(solution)/shard_map/all_to_all | solution.py:182
  134.6 16.0 %all_to_all.36 = bf16[8,64,256]{2,1,0:T(8,128)(2,1)S(1)} all-to-all(bf16[8,64,256]{2,1,0:T(8,128)(2,1)S(1)} %bitcast.46), channel_id=1, replica_groups=mesh['zh'=4,'core'=2,'zl'=2,'xh'=2,'xl'=2,'y'=8] {'y'}, dimensions={0} | all-to-all | bytes 524288 | tf_op jit(solution)/shard_map/all_to_all | solution.py:184
  (58 shorter events, 16.8 us)
Async XLA Ops:
  0.0 27.7 %all-to-all-start = ((bf16[8,2,128,128]{3,2,1,0:T(8,128)(2,1)}), bf16[8,2,128,128]{3,2,1,0:T(8,128)(2,1)S(1)}, u32[]{:S(2)}, u32[]{:S(2)}) async-start(bf16[8,2,128,128]{3,2,1,0:T(8,128)(2,1)} %bitcast.42), calls=%async_computation | async-start | bytes 1048576 | tf_op jit(solution)/shard_map/all_to_all | solution.py:145
  10.1 10.8 %collective-permute-start = (bf16[2,64,256]{2,1,0:T(8,128)(2,1)}, bf16[2,64,256]{2,1,0:T(8,128)(2,1)S(1)}, u32[]{:S(2)}, u32[]{:S(2)}) collective-permute-start(bf16[2,64,256]{2,1,0:T(8,128)(2,1)} %get-tuple-element.14), channel_id=1, source_target_pairs={{0,16},{16,0},{32,48},{48,32},{1,17},{17,1},{33,49},{49,33},{2,18}... | collective-permute-start | bytes 196616 | tf_op jit(solution)/shard_map/ppermute | solution.py:150
  15.5 6.4 %collective-permute-start.1 = (bf16[2,64,256]{2,1,0:T(8,128)(2,1)}, bf16[2,64,256]{2,1,0:T(8,128)(2,1)S(1)}, u32[]{:S(2)}, u32[]{:S(2)}) collective-permute-start(bf16[2,64,256]{2,1,0:T(8,128)(2,1)} %get-tuple-element.15), channel_id=1, source_target_pairs={{0,32},{16,48},{32,0},{48,16},{1,33},{17,49},{33,1},{49,17},{2,34}... | collective-permute-start | bytes 196616 | tf_op jit(solution)/shard_map/ppermute | solution.py:150
  18.9 8.8 %collective-permute-start.2 = (bf16[2,64,256]{2,1,0:T(8,128)(2,1)}, bf16[2,64,256]{2,1,0:T(8,128)(2,1)S(1)}, u32[]{:S(2)}, u32[]{:S(2)}) collective-permute-start(bf16[2,64,256]{2,1,0:T(8,128)(2,1)} %get-tuple-element.16), channel_id=1, source_target_pairs={{0,48},{16,32},{32,16},{48,0},{1,49},{17,33},{33,17},{49,1},{2,50}... | collective-permute-start | bytes 196616 | tf_op jit(solution)/shard_map/ppermute | solution.py:150
  20.9 6.8 %copy-start.7 = (bf16[2,64,256]{2,1,0:T(8,128)(2,1)}, bf16[2,64,256]{2,1,0:T(8,128)(2,1)S(1)}, u32[]{:S(2)}) copy-start(bf16[2,64,256]{2,1,0:T(8,128)(2,1)S(1)} %collective-permute-done.refs_1_) | copy-start | bytes 196612
  21.9 5.8 %copy-start.8 = (bf16[2,64,256]{2,1,0:T(8,128)(2,1)}, bf16[2,64,256]{2,1,0:T(8,128)(2,1)S(1)}, u32[]{:S(2)}) copy-start(bf16[2,64,256]{2,1,0:T(8,128)(2,1)S(1)} %collective-permute-done.1.refs_2_) | copy-start | bytes 196612
  27.7 0.8 copy-start
  30.3 51.2 %copy-start.10 = (f32[4096]{0:T(1024)S(1)}, f32[4096]{0:T(1024)}, u32[]{:S(2)}) copy-start(f32[4096]{0:T(1024)} %param.7) | copy-start | bytes 49156
  30.3 32.5 %all-to-all-start.1 = ((bf16[8,2,64,256]{3,2,1,0:T(8,128)(2,1)}), bf16[8,2,64,256]{3,2,1,0:T(8,128)(2,1)S(1)}, u32[]{:S(2)}, u32[]{:S(2)}) async-start(bf16[8,2,64,256]{3,2,1,0:T(8,128)(2,1)} %get-tuple-element.18), calls=%async_computation.1 | async-start | bytes 1048576 | tf_op jit(solution)/shard_map/all_to_all | solution.py:152
  38.0 6.4 %collective-permute-start.3 = (bf16[2,64,256]{2,1,0:T(8,128)(2,1)}, bf16[2,64,256]{2,1,0:T(8,128)(2,1)S(1)}, u32[]{:S(2)}, u32[]{:S(2)}) collective-permute-start(bf16[2,64,256]{2,1,0:T(8,128)(2,1)} %get-tuple-element.17.own_ref), channel_id=1, source_target_pairs={{0,8},{8,0},{1,9},{9,1},{2,10},{10,2},{3,11},{11,3},{4,12},{12,4},... | collective-permute-start | bytes 196616 | tf_op jit(solution)/shard_map/ppermute | solution.py:154
  44.4 18.4 %copy-start.4 = (bf16[2,64,256]{2,1,0:T(8,128)(2,1)}, bf16[2,64,256]{2,1,0:T(8,128)(2,1)S(1)}, u32[]{:S(2)}) copy-start(bf16[2,64,256]{2,1,0:T(8,128)(2,1)S(1)} %collective-permute-done.3.one_ref) | copy-start | bytes 196612
  45.3 8.4 %collective-permute-start.4 = (bf16[2,2,64,256]{3,2,1,0:T(8,128)(2,1)S(1)}, bf16[2,2,64,256]{3,2,1,0:T(8,128)(2,1)S(1)}, u32[]{:S(2)}, u32[]{:S(2)}) collective-permute-start(bf16[2,2,64,256]{3,2,1,0:T(8,128)(2,1)S(1)} %pad_maximum_fusion.2), channel_id=1, source_target_pairs={{0,16},{16,0},{1,17},{17,1},{2,18},{18,2},{3,19},{19,3},{4,20},{20... | collective-permute-start | bytes 393224 | tf_op jit(solution)/shard_map/ppermute | solution.py:156
  53.6 9.2 %copy-start.5 = (bf16[2,2,64,256]{3,2,1,0:T(8,128)(2,1)}, bf16[2,2,64,256]{3,2,1,0:T(8,128)(2,1)S(1)}, u32[]{:S(2)}) copy-start(bf16[2,2,64,256]{3,2,1,0:T(8,128)(2,1)S(1)} %collective-permute-done.4.two_ref) | copy-start | bytes 393220
  54.5 8.3 %collective-permute-start.5 = (bf16[4,2,64,256]{3,2,1,0:T(8,128)(2,1)S(1)}, bf16[4,2,64,256]{3,2,1,0:T(8,128)(2,1)S(1)}, u32[]{:S(2)}, u32[]{:S(2)}) collective-permute-start(bf16[4,2,64,256]{3,2,1,0:T(8,128)(2,1)S(1)} %pad_maximum_fusion.1), channel_id=1, source_target_pairs={{0,32},{32,0},{1,33},{33,1},{2,34},{34,2},{3,35},{35,3},{4,36},{36... | collective-permute-start | bytes 786440 | tf_op jit(solution)/shard_map/ppermute | solution.py:157
  62.8 0.7 copy-start.6
  63.5 0.8 copy-start.2
  66.8 3.6 %collective-permute-start.6 = (bf16[256,512]{1,0:T(8,128)(2,1)}, bf16[256,512]{1,0:T(8,128)(2,1)S(1)}, u32[]{:S(2)}, u32[]{:S(2)}) collective-permute-start(bf16[256,512]{1,0:T(8,128)(2,1)} %get-tuple-element.20), channel_id=1, source_target_pairs={{0,64},{64,0},{1,65},{65,1},{2,66},{66,2},{3,67},{67,3},{4,68},{68... | collective-permute-start | bytes 786440 | tf_op jit(solution)/shard_map/ppermute | solution.py:162
  72.1 20.2 %all-to-all-start.2 = ((bf16[4,64,512]{2,1,0:T(8,128)(2,1)}), bf16[4,64,512]{2,1,0:T(8,128)(2,1)S(1)}, u32[]{:S(2)}, u32[]{:S(2)}) async-start(bf16[4,64,512]{2,1,0:T(8,128)(2,1)} %bitcast.13), calls=%async_computation.2 | async-start | bytes 524288 | tf_op jit(solution)/shard_map/all_to_all | solution.py:164
  81.6 28.3 %slice-start = ((bf16[8,2,64,256]{3,2,1,0:T(8,128)(2,1)}), bf16[8,1,64,256]{3,2,1,0:T(8,128)(2,1)S(1)}, s32[]{:S(2)}) async-start(bf16[8,2,64,256]{3,2,1,0:T(8,128)(2,1)} %copy-done.2), calls=%async_computation.7 | async-start | bytes 524288 | tf_op jit(solution)/shard_map/slice | solution.py:175
  106.4 3.4 %collective-permute-start.7 = (bf16[4,64,512]{2,1,0:T(8,128)(2,1)S(1)}, bf16[4,64,512]{2,1,0:T(8,128)(2,1)S(1)}, u32[]{:S(2)}, u32[]{:S(2)}) collective-permute-start(bf16[4,64,512]{2,1,0:T(8,128)(2,1)S(1)} %all_to_all.35), channel_id=1, source_target_pairs={{0,64},{64,0},{1,65},{65,1},{2,66},{66,2},{3,67},{67,3},{4,68},{68... | collective-permute-start | bytes 786440 | tf_op jit(solution)/shard_map/ppermute | solution.py:170
  108.3 14.1 %copy-start.3 = (bf16[2,64,256]{2,1,0:T(8,128)(2,1)S(1)}, bf16[2,64,256]{2,1,0:T(8,128)(2,1)}, u32[]{:S(2)}) copy-start(bf16[2,64,256]{2,1,0:T(8,128)(2,1)} %get-tuple-element.17.own_ref) | copy-start | bytes 196612
  109.8 16.8 %copy-start.1 = (bf16[8,2,128,128]{3,2,1,0:T(8,128)(2,1)S(1)}, bf16[8,2,128,128]{3,2,1,0:T(8,128)(2,1)}, u32[]{:S(2)}) copy-start(bf16[8,2,128,128]{3,2,1,0:T(8,128)(2,1)} %copy-done) | copy-start | bytes 1572868
  110.9 11.5 %all-to-all-start.4 = ((bf16[8,64,256]{2,1,0:T(8,128)(2,1)}), bf16[8,64,256]{2,1,0:T(8,128)(2,1)S(1)}, u32[]{:S(2)}, u32[]{:S(2)}) async-start(bf16[8,64,256]{2,1,0:T(8,128)(2,1)} %bitcast.16), calls=%async_computation.4 | async-start | bytes 524288 | tf_op jit(solution)/shard_map/all_to_all | solution.py:178
  123.2 10.9 %all-to-all-start.5 = ((bf16[8,64,256]{2,1,0:T(8,128)(2,1)}), bf16[8,64,256]{2,1,0:T(8,128)(2,1)S(1)}, u32[]{:S(2)}, u32[]{:S(2)}) async-start(bf16[8,64,256]{2,1,0:T(8,128)(2,1)} %broadcast_in_dim.8), calls=%async_computation.5 | async-start | bytes 524288 | tf_op jit(solution)/shard_map/all_to_all | solution.py:182
  (1 other events, 0.6 us)

commit v3 on v1

v3 whole, which is shorter than its diff:
```python
import jax
import jax.numpy as jnp
from jax import lax
from jax.experimental import pallas as pl
from jax.experimental.pallas import tpu as pltpu
from jax.sharding import Mesh
from jax.sharding import PartitionSpec as P

F32 = jnp.float32
BF16 = jnp.bfloat16
AXES = ("zh", "core", "zl", "xh", "xl", "y")
SIZES = (4, 2, 2, 2, 2, 8)
ROWS = ("zl", "xh")
COLS = ("xl", "zl", "xh")
PLANE = ("zl", "xh", "xl")
LINE = ("xh", "xl")
SWAP = [(0, 1), (1, 0)]

IN_SMEM = pl.BlockSpec(memory_space=pltpu.SMEM)
ANYWHERE = pl.BlockSpec(memory_space=pl.ANY)
IN_VMEM = pl.BlockSpec(memory_space=pltpu.VMEM)


def call(kernel, scalars, arrays, outs, scratch=(), after=()):
    held = [pltpu.with_memory_space_constraint(a, pltpu.VMEM) for a in arrays]
    single = not isinstance(outs, (list, tuple))
    shapes = [outs] if single else outs
    got = pl.pallas_call(
        kernel,
        out_shape=[pltpu.VMEM(s, d) for s, d in shapes_of(shapes)],
        in_specs=[IN_SMEM] * len(scalars) + [IN_VMEM] * len(held) + [ANYWHERE] * len(after),
        out_specs=[IN_VMEM] * len(shapes),
        scratch_shapes=list(scratch),
    )(*scalars, *held, *after)
    return got[0] if single else got


def shapes_of(outs):
    return [(o.shape, o.dtype) for o in outs]


def out(dtype, *shape):
    return jax.ShapeDtypeStruct(shape, dtype)


def project_kernel(r_ref, x_ref, y_ref, eig_ref, out_ref, xs, tiles, sems, tile_sem):
    steps = eig_ref.shape[0]
    grid_rows = x_ref.shape[1] // (steps * 128)
    r = r_ref[0]

    def copy(s, la):
        src = x_ref if s == 0 else y_ref
        start = pl.multiple_of((la * grid_rows + r) * 128, 128)
        return pltpu.make_async_copy(
            src.at[:, pl.ds(start, 128)], xs.at[s, :, pl.ds(la * 128, 128)], sems.at[s, la]
        )

    load = pltpu.make_async_copy(eig_ref, tiles, tile_sem)
    load.start()
    for s in range(2):
        for la in range(steps):
            copy(s, la).start()
    load.wait()
    basis = jnp.concatenate(
        [tiles[:, lb].reshape(steps * 128, 128) for lb in range(tiles.shape[1])], 1
    )
    for s in range(2):
        for la in range(steps):
            copy(s, la).wait()
        part = jnp.dot(xs[s], basis, preferred_element_type=F32)
        turned = part.T.astype(BF16)
        out_ref[:, s] = turned.reshape(out_ref.shape[0], *out_ref.shape[2:])


def project(r, inputs, upstream, eig):
    tokens = inputs.shape[0]
    steps = eig.shape[0]
    return pl.pallas_call(
        project_kernel,
        out_shape=pltpu.VMEM((4, 2, 64, tokens), BF16),
        in_specs=[IN_SMEM, ANYWHERE, ANYWHERE, ANYWHERE],
        out_specs=IN_VMEM,
        scratch_shapes=[
            pltpu.VMEM((2, tokens, steps * 128), BF16),
            pltpu.VMEM(eig.shape, BF16),
            pltpu.SemaphoreType.DMA((2, steps)),
            pltpu.SemaphoreType.DMA,
        ],
        name="project",
    )(r, inputs, upstream, eig)


def spread_kernel(parts_ref, own_ref, copies_ref):
    total = parts_ref[0].astype(F32)
    for k in range(1, parts_ref.shape[0]):
        total += parts_ref[k].astype(F32)
    own = total.astype(BF16)
    own_ref[...] = own
    for k in range(copies_ref.shape[0]):
        copies_ref[k] = own


def gram_kernel(at_ref, *refs):
    pieces, (a_ref, *rest) = refs[:8], refs[8:]
    out_ref, left = rest[-2:]
    half, here = at_ref[0], at_ref[1]
    n = a_ref.shape[0] * a_ref.shape[2]
    tokens = a_ref.shape[3]
    apart = half ^ (here // 4)
    for group in range(2):

        @pl.when(apart == group)
        def _():
            for k in range(4):
                left[(here % 4) ^ k] = pieces[group * 4 + k][...]

    over = (((1,), (1,)), ((), ()))
    right_in = a_ref[:, 0].reshape(n, tokens)
    right_up = a_ref[:, 1].reshape(n, tokens)
    block = lax.dot_general(
        left[:, 0].reshape(256, tokens), right_up, over, preferred_element_type=F32
    )
    block += lax.dot_general(
        left[:, 1].reshape(256, tokens), right_in, over, preferred_element_type=F32
    )
    out_ref[...] = block.astype(BF16)


def add_kernel(a_ref, b_ref, out_ref):
    total = a_ref[...].astype(F32) + b_ref[...].astype(F32)
    out_ref[...] = total.astype(BF16).reshape(out_ref.shape)


def weigh_kernel(parts_ref, rows_ref, cols_ref, *rest):
    out_ref = rest[-1]
    share = parts_ref[0].astype(F32)
    for k in range(1, parts_ref.shape[0]):
        share += parts_ref[k].astype(F32)
    s_b = jnp.sqrt(rows_ref[...])
    s_a = jnp.sqrt(cols_ref[...])
    kernel = -1.0 / (s_b * s_a * (s_b + s_a))
    part = (kernel * (0.5 * share)).astype(BF16)
    for k in range(out_ref.shape[0]):
        out_ref[k] = part


def mix_kernel(core_ref, mine_ref, theirs_ref, a_ref, out_ref):
    core = core_ref[0]
    tokens = a_ref.shape[3]
    proj_in = a_ref[:, 0].reshape(-1, tokens)
    for half, ref in ((core, mine_ref), (1 - core, theirs_ref)):
        part = jnp.dot(ref[...].reshape(256, -1), proj_in, preferred_element_type=F32)
        out_ref[pl.ds(half * 4, 4)] = part.astype(BF16).reshape(4, 64, tokens)


def update_kernel(factor, parts_ref, own_ref, lam_ref, out_ref):
    mixed = parts_ref[0].astype(F32)
    for k in range(1, parts_ref.shape[0]):
        mixed += parts_ref[k].astype(F32)
    update = own_ref[1].astype(F32) / jnp.sqrt(lam_ref[...]) + factor * mixed
    update = update.astype(BF16)
    for k in range(out_ref.shape[0]):
        out_ref[k] = update


def assemble_kernel(at_ref, pair_ref, *refs):
    xh, xl = at_ref[0], at_ref[1]
    *got_refs, out_ref = refs
    here = xh * 2 + xl
    for k in range(4):
        piece = pair_ref.at[:, here] if k == 0 else got_refs[k - 1]
        there_h, there_l = xh ^ (k >> 1), xl ^ (k & 1)
        for zl in range(2):
            block = jnp.concatenate([piece[zl, 0], piece[zl, 1]], 1)
            cols = pl.ds(pl.multiple_of(there_l * 256, 256), 256)
            out_ref[zl * 2 + there_h, :, cols] = block


def finish_kernel(basis_ref, every_ref, out_ref):
    tokens = every_ref.shape[2]
    part = jnp.dot(
        basis_ref[...].reshape(512, 512),
        every_ref[...].reshape(512, tokens),
        preferred_element_type=F32,
    )
    out_ref[...] = part.astype(BF16).reshape(out_ref.shape)


def scalars(*values):
    return jnp.stack(values).astype(jnp.int32)


def on_device(inputs, upstream, eig_tiles, eigvals):
    zl, xh, xl, y = (lax.axis_index(a) for a in ("zl", "xh", "xl", "y"))
    zh, core = lax.axis_index("zh"), lax.axis_index("core")
    tokens = inputs.shape[0]
    eig = eig_tiles[0]
    r = zl * 2 + xh
    here = xl * 4 + r

    by_b = lax.dynamic_index_in_dim(eigvals.reshape(2, 2, 8, 128), y, 2, keepdims=False)
    lam_b = jnp.transpose(by_b, (1, 0, 2)).reshape(8, 64)
    cube = jnp.transpose(eigvals.reshape(2, 2, 8, 2, 64), (0, 3, 1, 2, 4)).reshape(8, 8, 64)
    lam_a = lax.dynamic_index_in_dim(cube, r * 2 + xl, 0, keepdims=False)
    lam_own = lax.dynamic_index_in_dim(lam_a, y, 0, keepdims=False).reshape(64, 1)
    lam_rows = lax.dynamic_index_in_dim(lam_b, core * 4 + zh, 0, keepdims=False).reshape(64, 1)
    lam_cols = lam_a.reshape(1, 512)

    parts = project(scalars(r), inputs, upstream, eig)
    got = lax.all_to_all(parts, ROWS, 0, 0, tiled=True)
    own, copies = call(
        spread_kernel, (), (got,), (out(BF16, 2, 64, tokens), out(BF16, 8, 2, 64, tokens))
    )
    right = lax.all_to_all(copies, "y", 0, 0, tiled=True)
    pieces = [own]
    for k in range(1, 8):
        p = (k >> 1) * 2 % 4 * 2 + (k & 1) * 2 + (k >> 2)
        pieces.append(lax.ppermute(own, PLANE, [(i, i ^ p) for i in range(8)]))

    halves = eig.reshape(2, 4, 2, 128, 128)
    away = lax.dynamic_index_in_dim(halves, 1 - zl, 0, keepdims=False)
    kept = lax.dynamic_index_in_dim(halves, zl, 0, keepdims=False)
    came = lax.ppermute(away, "zl", SWAP)
    pair = jnp.where(zl == 0, jnp.stack([kept, came]), jnp.stack([came, kept]))

    half_block = out(BF16, 256, 512)
    room = [pltpu.VMEM((4, 2, 64, tokens), BF16)]
    send = call(
        gram_kernel, (scalars(1 - core, here),), (*pieces, right), half_block, room, (came,)
    )
    other = lax.ppermute(send, "core", SWAP)
    keep = call(gram_kernel, (scalars(core, here),), (*pieces, right), half_block, room)
    both = call(add_kernel, (), (keep, other), out(BF16, 4, 64, 512))

    line = xh * 2 + xl
    near = []
    for k in range(1, 4):
        chunk = lax.dynamic_index_in_dim(pair, line ^ k, 1, keepdims=False)
        near.append(lax.ppermute(chunk, LINE, [(i, i ^ k) for i in range(4)]))

    shares = lax.all_to_all(both, "zh", 0, 0, tiled=True)
    part = call(
        weigh_kernel, (), (shares, lam_rows, lam_cols), out(BF16, 4, 64, 512), (), tuple(near)
    )
    mine = lax.all_to_all(part, "zh", 0, 0, tiled=True)
    theirs = lax.ppermute(mine, "core", SWAP)
    mixed_part = call(mix_kernel, (scalars(core),), (mine, theirs, right), out(BF16, 8, 64, tokens))
    basis_rows = call(assemble_kernel, (scalars(xh, xl),), (pair, *near), out(BF16, 4, 128, 512))
    mixed = lax.all_to_all(mixed_part, COLS, 0, 0, tiled=True)
    factor = 2.0 / (8 * tokens)
    update = call(
        lambda *refs: update_kernel(factor, *refs),
        (),
        (mixed, own, lam_own),
        out(BF16, 8, 64, tokens),
    )
    every = lax.all_to_all(update, COLS, 0, 0, tiled=True)
    grad_part = call(finish_kernel, (), (basis_rows, every), out(BF16, 8, 64, tokens))
    blocks = lax.all_to_all(grad_part, "y", 0, 0, tiled=True)
    return jnp.sum(blocks.astype(F32), 0).astype(BF16)


def solution(mesh):
    grid = Mesh(mesh.devices.reshape(SIZES), AXES)
    dp, mp = AXES[:2], AXES[2:]
    return jax.shard_map(
        on_device,
        mesh=grid,
        in_specs=(P(dp, None), P(dp, None), P(mp, None, None, None, None), P()),
        out_specs=P(mp, dp),
        check_vma=False,
    )
```

time: 149 us -> 148 us (level)
  starting transfers between devices: 23.6 us -> 65.1 us
  blocking collectives: 73.2 us -> 46.4 us
  waiting for transfers between devices: 37.8 us -> 21.4 us
  Pallas kernels: 6.31 us -> 9.31 us
  local copies, waits for them, and re-layouts: 3.54 us -> 1.23 us
    ppermute x2 -> x13, starting transfers between devices: 3.82 us -> 40.5 us  [the longest x7 23.9 us: on_device(): pieces.append(lax.ppermute(own, PLANE, [(i, i ^ p) for i in range(8)]))]
    all_to_all x4 -> x2, blocking collectives: 59.8 us -> 33.1 us  [the longest x1 17.2 us: on_device(): mine = lax.all_to_all(part, 'zh', 0, 0, tiled=True)]
    all_to_all x4, waiting for transfers between devices: 34.6 us -> 13.9 us  [the longest x1 7.76 us: on_device(): mixed = lax.all_to_all(mixed_part, COLS, 0, 0, tiled=True)]
    all_to_all x4, starting transfers between devices: 19.8 us -> 24.6 us  [the longest x1 9.4 us: on_device(): shares = lax.all_to_all(both, 'zh', 0, 0, tiled=True)]
    ppermute x2 -> x13, waiting for transfers between devices: 3.21 us -> 7.55 us  [the longest x3 3.92 us: on_device(): near.append(lax.ppermute(chunk, LINE, [(i, i ^ k) for i in range(4)]))]
    pallas_call x2 -> x10, Pallas kernels: 6.31 us -> 9.31 us  [the longest x9 6.64 us: call(): pl.pallas_call(kernel, out_shape=[pltpu.VMEM(s, d) for s, d in shapes_of(...]
    another operation x0 -> x3, other arithmetic: none -> 1.97 us  [scalars(): return jnp.stack(values).astype(jnp.int32)]
    convert_element_type x2 -> x0, other arithmetic: 1.81 us -> none  [the longest x1 1.71 us: on_device(): (keep.astype(F32) + other.astype(F32)).astype(BF16).reshape(4, 64, 512)]
  transfers between devices with their start and end apart: 6 -> 17, of which waited for: 6 -> 7; matrix products, arithmetic and copies ran while one was open for 1% -> 2% of each run, Pallas kernels for 0% -> 1%
where the time goes in v3:
time: 148 us; the launch traced here: 147 us
  starting transfers between devices  65.1 us (44%)
  blocking collectives  46.4 us (31%)
  waiting for transfers between devices  21.4 us (14%)
  Pallas kernels  9.31 us (6%)
  other arithmetic  2.7 us (2%)
    ppermute x7, starting transfers between devices, on_device(): pieces.append(lax.ppermute(own, PLANE, [(i, i ^ p) for i in range(8)]))  23.9 us
    all_to_all x1, blocking collectives, on_device(): mine = lax.all_to_all(part, 'zh', 0, 0, tiled=True)  17.2 us
    all_to_all x1, blocking collectives, on_device(): blocks = lax.all_to_all(grad_part, 'y', 0, 0, tiled=True)  15.9 us
    all_to_all x1, blocking collectives, on_device(): got = lax.all_to_all(parts, ROWS, 0, 0, tiled=True)  13.3 us
    ppermute x3, starting transfers between devices, on_device(): near.append(lax.ppermute(chunk, LINE, [(i, i ^ k) for i in range(4)]))  9.82 us
    all_to_all x1, starting transfers between devices, on_device(): shares = lax.all_to_all(both, 'zh', 0, 0, tiled=True)  9.4 us
    all_to_all x1, waiting for transfers between devices, on_device(): mixed = lax.all_to_all(mixed_part, COLS, 0, 0, tiled=True)  7.76 us
    all_to_all x1, starting transfers between devices, on_device(): right = lax.all_to_all(copies, 'y', 0, 0, tiled=True)  7.55 us
  transfers between devices with their start and end apart: 17, of which 7 were waited for; matrix products, arithmetic and copies ran while one was open for 2% of the time, Pallas kernels for 1%

profile of v3, /device:TPU:8, one launch (start us, length us, event | category | flops | bytes accessed | tf_op | source)
XLA Modules:
  0.0 146.5 jit_solution(9958125773568400529)
XLA Ops:
  0.0 2.7 %project.1 = bf16[4,2,64,256]{3,2,1,0:T(8,128)(2,1)S(1)} custom-call(s32[1]{0:T(128)} %bitcast.10.r_ref, bf16[256,4096]{1,0:T(8,128)(2,1)} %x_ref.1, bf16[256,4096]{1,0:T(8,128)(2,1)} %y_ref.1, bf16[8,2,128,128]{3,2,1,0:T(8,128)(2,1)} %bitcast.27), custom_call_target="tpu_custom_call" | custom-call | tf_op jit(solution)/shard_map/project/pallas_call | solution.py:78
  2.7 13.3 %all_to_all.35.parts_ref = bf16[4,2,64,256]{3,2,1,0:T(8,128)(2,1)S(1)} all-to-all(bf16[4,2,64,256]{3,2,1,0:T(8,128)(2,1)S(1)} %project.1), channel_id=1, replica_groups=mesh['zh'=4,'core'=2,'zl'=2,'xh'=2,'xl'=2,'y'=8] {'zl','xh'}, dimensions={0} | all-to-all | bytes 524288 | tf_op jit(solution)/shard_map/all_to_all | solution.py:210
  16.8 7.5 %all-to-all-start.1 = ((bf16[8,2,64,256]{3,2,1,0:T(8,128)(2,1)}), bf16[8,2,64,256]{3,2,1,0:T(8,128)(2,1)S(1)}, u32[]{:S(2)}, u32[]{:S(2)}) async-start(bf16[8,2,64,256]{3,2,1,0:T(8,128)(2,1)} %get-tuple-element.8), calls=%async_computation.1 | async-start | bytes 1048576 | tf_op jit(solution)/shard_map/all_to_all | solution.py:214
  24.4 2.8 %collective-permute-start = (bf16[4,2,128,128]{3,2,1,0:T(8,128)(2,1)S(1)}, bf16[4,2,128,128]{3,2,1,0:T(8,128)(2,1)S(1)}, u32[]{:S(2)}, u32[]{:S(2)}) collective-permute-start(bf16[4,2,128,128]{3,2,1,0:T(8,128)(2,1)S(1)} %get-tuple-element.13), channel_id=1, source_target_pairs={{0,32},{32,0},{1,33},{33,1},{2,34},{34,2},{3,35},{35,3},{4,36},{36... | collective-permute-start | bytes 786440 | tf_op jit(solution)/shard_map/ppermute | solution.py:223
  27.2 3.1 %collective-permute-start.10 = (bf16[2,64,256]{2,1,0:T(8,128)(2,1)S(1)}, bf16[2,64,256]{2,1,0:T(8,128)(2,1)S(1)}, u32[]{:S(2)}, u32[]{:S(2)}) collective-permute-start(bf16[2,64,256]{2,1,0:T(8,128)(2,1)S(1)} %get-tuple-element.7.refs_0_.refs_1_), channel_id=1, source_target_pairs={{0,56},{8,48},{16,40},{24,32},{32,24},{40,16},{48,8},{56,0},{1,57}... | collective-permute-start | bytes 196616 | tf_op jit(solution)/shard_map/ppermute | solution.py:218
  30.4 2.1 %collective-permute-start.9 = (bf16[2,64,256]{2,1,0:T(8,128)(2,1)S(1)}, bf16[2,64,256]{2,1,0:T(8,128)(2,1)S(1)}, u32[]{:S(2)}, u32[]{:S(2)}) collective-permute-start(bf16[2,64,256]{2,1,0:T(8,128)(2,1)S(1)} %get-tuple-element.7.refs_0_.refs_1_), channel_id=1, source_target_pairs={{0,40},{8,32},{16,56},{24,48},{32,8},{40,0},{48,24},{56,16},{1,41}... | collective-permute-start | bytes 196616 | tf_op jit(solution)/shard_map/ppermute | solution.py:218
  32.5 4.6 %collective-permute-start.8 = (bf16[2,64,256]{2,1,0:T(8,128)(2,1)S(1)}, bf16[2,64,256]{2,1,0:T(8,128)(2,1)S(1)}, u32[]{:S(2)}, u32[]{:S(2)}) collective-permute-start(bf16[2,64,256]{2,1,0:T(8,128)(2,1)S(1)} %get-tuple-element.7.refs_0_.refs_1_), channel_id=1, source_target_pairs={{0,24},{8,16},{16,8},{24,0},{32,56},{40,48},{48,40},{56,32},{1,25}... | collective-permute-start | bytes 196616 | tf_op jit(solution)/shard_map/ppermute | solution.py:218
  37.1 3.3 %collective-permute-start.7 = (bf16[2,64,256]{2,1,0:T(8,128)(2,1)S(1)}, bf16[2,64,256]{2,1,0:T(8,128)(2,1)S(1)}, u32[]{:S(2)}, u32[]{:S(2)}) collective-permute-start(bf16[2,64,256]{2,1,0:T(8,128)(2,1)S(1)} %get-tuple-element.7.refs_0_.refs_1_), channel_id=1, source_target_pairs={{0,8},{8,0},{16,24},{24,16},{32,40},{40,32},{48,56},{56,48},{1,9},... | collective-permute-start | bytes 196616 | tf_op jit(solution)/shard_map/ppermute | solution.py:218
  40.5 3.4 %collective-permute-start.6 = (bf16[2,64,256]{2,1,0:T(8,128)(2,1)S(1)}, bf16[2,64,256]{2,1,0:T(8,128)(2,1)S(1)}, u32[]{:S(2)}, u32[]{:S(2)}) collective-permute-start(bf16[2,64,256]{2,1,0:T(8,128)(2,1)S(1)} %get-tuple-element.7.refs_0_.refs_1_), channel_id=1, source_target_pairs={{0,48},{8,56},{16,32},{24,40},{32,16},{40,24},{48,0},{56,8},{1,49}... | collective-permute-start | bytes 196616 | tf_op jit(solution)/shard_map/ppermute | solution.py:218
  43.9 2.5 %collective-permute-start.5 = (bf16[2,64,256]{2,1,0:T(8,128)(2,1)S(1)}, bf16[2,64,256]{2,1,0:T(8,128)(2,1)S(1)}, u32[]{:S(2)}, u32[]{:S(2)}) collective-permute-start(bf16[2,64,256]{2,1,0:T(8,128)(2,1)S(1)} %get-tuple-element.7.refs_0_.refs_1_), channel_id=1, source_target_pairs={{0,32},{8,40},{16,48},{24,56},{32,0},{40,8},{48,16},{56,24},{1,33}... | collective-permute-start | bytes 196616 | tf_op jit(solution)/shard_map/ppermute | solution.py:218
  46.4 4.9 %collective-permute-start.4 = (bf16[2,64,256]{2,1,0:T(8,128)(2,1)S(1)}, bf16[2,64,256]{2,1,0:T(8,128)(2,1)S(1)}, u32[]{:S(2)}, u32[]{:S(2)}) collective-permute-start(bf16[2,64,256]{2,1,0:T(8,128)(2,1)S(1)} %get-tuple-element.7.refs_0_.refs_1_), channel_id=1, source_target_pairs={{0,16},{8,24},{16,0},{24,8},{32,48},{40,56},{48,32},{56,40},{1,17}... | collective-permute-start | bytes 196616 | tf_op jit(solution)/shard_map/ppermute | solution.py:218
  51.9 2.1 %collective-permute-done.4.refs_1_ = bf16[2,64,256]{2,1,0:T(8,128)(2,1)S(1)} collective-permute-done((bf16[2,64,256]{2,1,0:T(8,128)(2,1)S(1)}, bf16[2,64,256]{2,1,0:T(8,128)(2,1)S(1)}, u32[]{:S(2)}, u32[]{:S(2)}) %collective-permute-start.4) | collective-permute-done | bytes 65568 | tf_op jit(solution)/shard_map/ppermute | solution.py:218
  55.1 2.1 %collective-permute-start.11 = (bf16[256,512]{1,0:T(8,128)(2,1)S(1)}, bf16[256,512]{1,0:T(8,128)(2,1)S(1)}, u32[]{:S(2)}, u32[]{:S(2)}) collective-permute-start(bf16[256,512]{1,0:T(8,128)(2,1)S(1)} %shard_map.49), channel_id=1, source_target_pairs={{0,64},{64,0},{1,65},{65,1},{2,66},{66,2},{3,67},{67,3},{4,68},{68... | collective-permute-start | bytes 786440 | tf_op jit(solution)/shard_map/ppermute | solution.py:231
  59.8 9.4 %all-to-all-start.2 = ((bf16[4,64,512]{2,1,0:T(8,128)(2,1)}), bf16[4,64,512]{2,1,0:T(8,128)(2,1)S(1)}, u32[]{:S(2)}, u32[]{:S(2)}) async-start(bf16[4,64,512]{2,1,0:T(8,128)(2,1)} %shard_map.50), calls=%async_computation.2 | async-start | bytes 524288 | tf_op jit(solution)/shard_map/all_to_all | solution.py:241
  69.3 4.6 %collective-permute-start.3 = (bf16[2,2,128,128]{3,2,1,0:T(8,128)(2,1)S(1)}, bf16[2,2,128,128]{3,2,1,0:T(8,128)(2,1)S(1)}, u32[]{:S(2)}, u32[]{:S(2)}) collective-permute-start(bf16[2,2,128,128]{3,2,1,0:T(8,128)(2,1)S(1)} %get-tuple-element.9), channel_id=1, source_target_pairs={{0,24},{8,16},{16,8},{24,0},{1,25},{9,17},{17,9},{25,1},{2,26},{10... | collective-permute-start | bytes 393224 | tf_op jit(solution)/shard_map/ppermute | solution.py:239
  73.9 2.2 %collective-permute-start.2 = (bf16[2,2,128,128]{3,2,1,0:T(8,128)(2,1)S(1)}, bf16[2,2,128,128]{3,2,1,0:T(8,128)(2,1)S(1)}, u32[]{:S(2)}, u32[]{:S(2)}) collective-permute-start(bf16[2,2,128,128]{3,2,1,0:T(8,128)(2,1)S(1)} %get-tuple-element.10), channel_id=1, source_target_pairs={{0,16},{8,24},{16,0},{24,8},{1,17},{9,25},{17,1},{25,9},{2,18},{10... | collective-permute-start | bytes 393224 | tf_op jit(solution)/shard_map/ppermute | solution.py:239
  76.1 3.0 %collective-permute-start.1 = (bf16[2,2,128,128]{3,2,1,0:T(8,128)(2,1)S(1)}, bf16[2,2,128,128]{3,2,1,0:T(8,128)(2,1)S(1)}, u32[]{:S(2)}, u32[]{:S(2)}) collective-permute-start(bf16[2,2,128,128]{3,2,1,0:T(8,128)(2,1)S(1)} %get-tuple-element.11), channel_id=1, source_target_pairs={{0,8},{8,0},{16,24},{24,16},{1,9},{9,1},{17,25},{25,17},{2,10},{10... | collective-permute-start | bytes 393224 | tf_op jit(solution)/shard_map/ppermute | solution.py:239
  79.9 3.1 %collective-permute-done.2.refs_1_.rest_1_ = bf16[2,2,128,128]{3,2,1,0:T(8,128)(2,1)S(1)} collective-permute-done((bf16[2,2,128,128]{3,2,1,0:T(8,128)(2,1)S(1)}, bf16[2,2,128,128]{3,2,1,0:T(8,128)(2,1)S(1)}, u32[]{:S(2)}, u32[]{:S(2)}) %collective-permute-start.2) | collective-permute-done | bytes 131104 | tf_op jit(solution)/shard_map/ppermute | solution.py:239
  84.2 17.2 %all_to_all.36.mine_ref = bf16[4,64,512]{2,1,0:T(8,128)(2,1)S(1)} all-to-all(bf16[4,64,512]{2,1,0:T(8,128)(2,1)S(1)} %shard_map.51), channel_id=1, replica_groups=mesh['zh'=4,'core'=2,'zl'=2,'xh'=2,'xl'=2,'y'=8] {'zh'}, dimensions={0} | all-to-all | bytes 524288 | tf_op jit(solution)/shard_map/all_to_all | solution.py:245
  105.8 4.2 %all-to-all-start.4 = ((bf16[8,64,256]{2,1,0:T(8,128)(2,1)}), bf16[8,64,256]{2,1,0:T(8,128)(2,1)S(1)}, u32[]{:S(2)}, u32[]{:S(2)}) async-start(bf16[8,64,256]{2,1,0:T(8,128)(2,1)} %shard_map.52), calls=%async_computation.4 | async-start | bytes 524288 | tf_op jit(solution)/shard_map/all_to_all | solution.py:249
  110.2 7.8 %all-to-all-done.4.refs_0_ = bf16[8,64,256]{2,1,0:T(8,128)(2,1)S(1)} async-done(((bf16[8,64,256]{2,1,0:T(8,128)(2,1)}), bf16[8,64,256]{2,1,0:T(8,128)(2,1)S(1)}, u32[]{:S(2)}, u32[]{:S(2)}) %all-to-all-start.4) | async-done | bytes 262176 | tf_op jit(solution)/shard_map/all_to_all | solution.py:249
  118.8 3.4 %all-to-all-start.5 = ((bf16[8,64,256]{2,1,0:T(8,128)(2,1)}), bf16[8,64,256]{2,1,0:T(8,128)(2,1)S(1)}, u32[]{:S(2)}, u32[]{:S(2)}) async-start(bf16[8,64,256]{2,1,0:T(8,128)(2,1)} %shard_map.53), calls=%async_computation.5 | async-start | bytes 524288 | tf_op jit(solution)/shard_map/all_to_all | solution.py:257
  123.6 6.1 %all-to-all-done.5.every_ref = bf16[8,64,256]{2,1,0:T(8,128)(2,1)S(1)} async-done(((bf16[8,64,256]{2,1,0:T(8,128)(2,1)}), bf16[8,64,256]{2,1,0:T(8,128)(2,1)S(1)}, u32[]{:S(2)}, u32[]{:S(2)}) %all-to-all-start.5) | async-done | bytes 262176 | tf_op jit(solution)/shard_map/all_to_all | solution.py:257
  130.0 15.9 %all_to_all.37 = bf16[8,64,256]{2,1,0:T(8,128)(2,1)S(1)} all-to-all(bf16[8,64,256]{2,1,0:T(8,128)(2,1)S(1)} %shard_map.54), channel_id=1, replica_groups=mesh['zh'=4,'core'=2,'zl'=2,'xh'=2,'xl'=2,'y'=8] {'y'}, dimensions={0} | all-to-all | bytes 524288 | tf_op jit(solution)/shard_map/all_to_all | solution.py:259
  (61 shorter events, 14.8 us)
Async XLA Ops:
  2.7 21.7 %copy-start.6 = (bf16[1,8,2,128,128]{4,3,2,1,0:T(8,128)(2,1)S(1)}, bf16[1,8,2,128,128]{4,3,2,1,0:T(8,128)(2,1)}, u32[]{:S(2)}) copy-start(bf16[1,8,2,128,128]{4,3,2,1,0:T(8,128)(2,1)} %param.6) | copy-start | bytes 1572868
  15.9 41.2 %copy-start.9 = (f32[4096]{0:T(1024)S(1)}, f32[4096]{0:T(1024)}, u32[]{:S(2)}) copy-start(f32[4096]{0:T(1024)} %param.7) | copy-start | bytes 49156
  16.8 37.2 %all-to-all-start.1 = ((bf16[8,2,64,256]{3,2,1,0:T(8,128)(2,1)}), bf16[8,2,64,256]{3,2,1,0:T(8,128)(2,1)S(1)}, u32[]{:S(2)}, u32[]{:S(2)}) async-start(bf16[8,2,64,256]{3,2,1,0:T(8,128)(2,1)} %get-tuple-element.8), calls=%async_computation.1 | async-start | bytes 1048576 | tf_op jit(solution)/shard_map/all_to_all | solution.py:214
  24.4 16.1 %collective-permute-start = (bf16[4,2,128,128]{3,2,1,0:T(8,128)(2,1)S(1)}, bf16[4,2,128,128]{3,2,1,0:T(8,128)(2,1)S(1)}, u32[]{:S(2)}, u32[]{:S(2)}) collective-permute-start(bf16[4,2,128,128]{3,2,1,0:T(8,128)(2,1)S(1)} %get-tuple-element.13), channel_id=1, source_target_pairs={{0,32},{32,0},{1,33},{33,1},{2,34},{34,2},{3,35},{35,3},{4,36},{36... | collective-permute-start | bytes 786440 | tf_op jit(solution)/shard_map/ppermute | solution.py:223
  27.2 16.6 %collective-permute-start.10 = (bf16[2,64,256]{2,1,0:T(8,128)(2,1)S(1)}, bf16[2,64,256]{2,1,0:T(8,128)(2,1)S(1)}, u32[]{:S(2)}, u32[]{:S(2)}) collective-permute-start(bf16[2,64,256]{2,1,0:T(8,128)(2,1)S(1)} %get-tuple-element.7.refs_0_.refs_1_), channel_id=1, source_target_pairs={{0,56},{8,48},{16,40},{24,32},{32,24},{40,16},{48,8},{56,0},{1,57}... | collective-permute-start | bytes 196616 | tf_op jit(solution)/shard_map/ppermute | solution.py:218
  30.4 16.0 %collective-permute-start.9 = (bf16[2,64,256]{2,1,0:T(8,128)(2,1)S(1)}, bf16[2,64,256]{2,1,0:T(8,128)(2,1)S(1)}, u32[]{:S(2)}, u32[]{:S(2)}) collective-permute-start(bf16[2,64,256]{2,1,0:T(8,128)(2,1)S(1)} %get-tuple-element.7.refs_0_.refs_1_), channel_id=1, source_target_pairs={{0,40},{8,32},{16,56},{24,48},{32,8},{40,0},{48,24},{56,16},{1,41}... | collective-permute-start | bytes 196616 | tf_op jit(solution)/shard_map/ppermute | solution.py:218
  32.5 19.4 %collective-permute-start.8 = (bf16[2,64,256]{2,1,0:T(8,128)(2,1)S(1)}, bf16[2,64,256]{2,1,0:T(8,128)(2,1)S(1)}, u32[]{:S(2)}, u32[]{:S(2)}) collective-permute-start(bf16[2,64,256]{2,1,0:T(8,128)(2,1)S(1)} %get-tuple-element.7.refs_0_.refs_1_), channel_id=1, source_target_pairs={{0,24},{8,16},{16,8},{24,0},{32,56},{40,48},{48,40},{56,32},{1,25}... | collective-permute-start | bytes 196616 | tf_op jit(solution)/shard_map/ppermute | solution.py:218
  37.1 14.8 %collective-permute-start.7 = (bf16[2,64,256]{2,1,0:T(8,128)(2,1)S(1)}, bf16[2,64,256]{2,1,0:T(8,128)(2,1)S(1)}, u32[]{:S(2)}, u32[]{:S(2)}) collective-permute-start(bf16[2,64,256]{2,1,0:T(8,128)(2,1)S(1)} %get-tuple-element.7.refs_0_.refs_1_), channel_id=1, source_target_pairs={{0,8},{8,0},{16,24},{24,16},{32,40},{40,32},{48,56},{56,48},{1,9},... | collective-permute-start | bytes 196616 | tf_op jit(solution)/shard_map/ppermute | solution.py:218
  40.5 13.6 %copy-start.7 = (bf16[4,2,128,128]{3,2,1,0:T(8,128)(2,1)}, bf16[4,2,128,128]{3,2,1,0:T(8,128)(2,1)S(1)}, u32[]{:S(2)}) copy-start(bf16[4,2,128,128]{3,2,1,0:T(8,128)(2,1)S(1)} %collective-permute-done.refs_9_) | copy-start | bytes 786436
  40.5 11.4 %collective-permute-start.6 = (bf16[2,64,256]{2,1,0:T(8,128)(2,1)S(1)}, bf16[2,64,256]{2,1,0:T(8,128)(2,1)S(1)}, u32[]{:S(2)}, u32[]{:S(2)}) collective-permute-start(bf16[2,64,256]{2,1,0:T(8,128)(2,1)S(1)} %get-tuple-element.7.refs_0_.refs_1_), channel_id=1, source_target_pairs={{0,48},{8,56},{16,32},{24,40},{32,16},{40,24},{48,0},{56,8},{1,49}... | collective-permute-start | bytes 196616 | tf_op jit(solution)/shard_map/ppermute | solution.py:218
  43.9 8.0 %collective-permute-start.5 = (bf16[2,64,256]{2,1,0:T(8,128)(2,1)S(1)}, bf16[2,64,256]{2,1,0:T(8,128)(2,1)S(1)}, u32[]{:S(2)}, u32[]{:S(2)}) collective-permute-start(bf16[2,64,256]{2,1,0:T(8,128)(2,1)S(1)} %get-tuple-element.7.refs_0_.refs_1_), channel_id=1, source_target_pairs={{0,32},{8,40},{16,48},{24,56},{32,0},{40,8},{48,16},{56,24},{1,33}... | collective-permute-start | bytes 196616 | tf_op jit(solution)/shard_map/ppermute | solution.py:218
  46.4 7.7 %collective-permute-start.4 = (bf16[2,64,256]{2,1,0:T(8,128)(2,1)S(1)}, bf16[2,64,256]{2,1,0:T(8,128)(2,1)S(1)}, u32[]{:S(2)}, u32[]{:S(2)}) collective-permute-start(bf16[2,64,256]{2,1,0:T(8,128)(2,1)S(1)} %get-tuple-element.7.refs_0_.refs_1_), channel_id=1, source_target_pairs={{0,16},{8,24},{16,0},{24,8},{32,48},{40,56},{48,32},{56,40},{1,17}... | collective-permute-start | bytes 196616 | tf_op jit(solution)/shard_map/ppermute | solution.py:218
  55.1 14.1 %copy-start.8 = (bf16[4,2,128,128]{3,2,1,0:T(8,128)(2,1)S(1)}, bf16[4,2,128,128]{3,2,1,0:T(8,128)(2,1)}, u32[]{:S(2)}) copy-start(bf16[4,2,128,128]{3,2,1,0:T(8,128)(2,1)} %copy-done.7) | copy-start | bytes 786436
  55.1 3.9 %collective-permute-start.11 = (bf16[256,512]{1,0:T(8,128)(2,1)S(1)}, bf16[256,512]{1,0:T(8,128)(2,1)S(1)}, u32[]{:S(2)}, u32[]{:S(2)}) collective-permute-start(bf16[256,512]{1,0:T(8,128)(2,1)S(1)} %shard_map.49), channel_id=1, source_target_pairs={{0,64},{64,0},{1,65},{65,1},{2,66},{66,2},{3,67},{67,3},{4,68},{68... | collective-permute-start | bytes 786440 | tf_op jit(solution)/shard_map/ppermute | solution.py:231
  59.8 23.6 %all-to-all-start.2 = ((bf16[4,64,512]{2,1,0:T(8,128)(2,1)}), bf16[4,64,512]{2,1,0:T(8,128)(2,1)S(1)}, u32[]{:S(2)}, u32[]{:S(2)}) async-start(bf16[4,64,512]{2,1,0:T(8,128)(2,1)} %shard_map.50), calls=%async_computation.2 | async-start | bytes 524288 | tf_op jit(solution)/shard_map/all_to_all | solution.py:241
  69.3 10.6 %collective-permute-start.3 = (bf16[2,2,128,128]{3,2,1,0:T(8,128)(2,1)S(1)}, bf16[2,2,128,128]{3,2,1,0:T(8,128)(2,1)S(1)}, u32[]{:S(2)}, u32[]{:S(2)}) collective-permute-start(bf16[2,2,128,128]{3,2,1,0:T(8,128)(2,1)S(1)} %get-tuple-element.9), channel_id=1, source_target_pairs={{0,24},{8,16},{16,8},{24,0},{1,25},{9,17},{17,9},{25,1},{2,26},{10... | collective-permute-start | bytes 393224 | tf_op jit(solution)/shard_map/ppermute | solution.py:239
  73.9 9.1 %collective-permute-start.2 = (bf16[2,2,128,128]{3,2,1,0:T(8,128)(2,1)S(1)}, bf16[2,2,128,128]{3,2,1,0:T(8,128)(2,1)S(1)}, u32[]{:S(2)}, u32[]{:S(2)}) collective-permute-start(bf16[2,2,128,128]{3,2,1,0:T(8,128)(2,1)S(1)} %get-tuple-element.10), channel_id=1, source_target_pairs={{0,16},{8,24},{16,0},{24,8},{1,17},{9,25},{17,1},{25,9},{2,18},{10... | collective-permute-start | bytes 393224 | tf_op jit(solution)/shard_map/ppermute | solution.py:239
  76.1 7.3 %collective-permute-start.1 = (bf16[2,2,128,128]{3,2,1,0:T(8,128)(2,1)S(1)}, bf16[2,2,128,128]{3,2,1,0:T(8,128)(2,1)S(1)}, u32[]{:S(2)}, u32[]{:S(2)}) collective-permute-start(bf16[2,2,128,128]{3,2,1,0:T(8,128)(2,1)S(1)} %get-tuple-element.11), channel_id=1, source_target_pairs={{0,8},{8,0},{16,24},{24,16},{1,9},{9,1},{17,25},{25,17},{2,10},{10... | collective-permute-start | bytes 393224 | tf_op jit(solution)/shard_map/ppermute | solution.py:239
  84.2 38.7 %copy-start.1 = (bf16[2,2,128,128]{3,2,1,0:T(8,128)(2,1)S(1)}, bf16[2,2,128,128]{3,2,1,0:T(8,128)(2,1)}, u32[]{:S(2)}) copy-start(bf16[2,2,128,128]{3,2,1,0:T(8,128)(2,1)} %copy-done) | copy-start | bytes 393220
  84.2 38.7 %copy-start.3 = (bf16[2,2,128,128]{3,2,1,0:T(8,128)(2,1)S(1)}, bf16[2,2,128,128]{3,2,1,0:T(8,128)(2,1)}, u32[]{:S(2)}) copy-start(bf16[2,2,128,128]{3,2,1,0:T(8,128)(2,1)} %copy-done.2) | copy-start | bytes 393220
  84.2 38.7 %copy-start.5 = (bf16[2,2,128,128]{3,2,1,0:T(8,128)(2,1)S(1)}, bf16[2,2,128,128]{3,2,1,0:T(8,128)(2,1)}, u32[]{:S(2)}) copy-start(bf16[2,2,128,128]{3,2,1,0:T(8,128)(2,1)} %copy-done.4) | copy-start | bytes 393220
  101.4 3.4 %collective-permute-start.12 = (bf16[4,64,512]{2,1,0:T(8,128)(2,1)S(1)}, bf16[4,64,512]{2,1,0:T(8,128)(2,1)S(1)}, u32[]{:S(2)}, u32[]{:S(2)}) collective-permute-start(bf16[4,64,512]{2,1,0:T(8,128)(2,1)S(1)} %all_to_all.36.mine_ref), channel_id=1, source_target_pairs={{0,64},{64,0},{1,65},{65,1},{2,66},{66,2},{3,67},{67,3},{4,68},{68... | collective-permute-start | bytes 786440 | tf_op jit(solution)/shard_map/ppermute | solution.py:246
  105.8 12.1 %all-to-all-start.4 = ((bf16[8,64,256]{2,1,0:T(8,128)(2,1)}), bf16[8,64,256]{2,1,0:T(8,128)(2,1)S(1)}, u32[]{:S(2)}, u32[]{:S(2)}) async-start(bf16[8,64,256]{2,1,0:T(8,128)(2,1)} %shard_map.52), calls=%async_computation.4 | async-start | bytes 524288 | tf_op jit(solution)/shard_map/all_to_all | solution.py:249
  118.8 10.9 %all-to-all-start.5 = ((bf16[8,64,256]{2,1,0:T(8,128)(2,1)}), bf16[8,64,256]{2,1,0:T(8,128)(2,1)S(1)}, u32[]{:S(2)}, u32[]{:S(2)}) async-start(bf16[8,64,256]{2,1,0:T(8,128)(2,1)} %shard_map.53), calls=%async_computation.5 | async-start | bytes 524288 | tf_op jit(solution)/shard_map/all_to_all | solution.py:257
  (3 other events, 4.8 us)
